TPU v7x, 8 devices: a whole 2x2x1 slice. The times are simulated.
8 devices in a mesh: dp: 2 (over z, y), fo: 2 (over x), fi: 2 (over core).
Axes of the slice: x: 2, y: 2, z: 1, core: 2. Of those that a mesh axis runs over, the one named last changes fastest.
Arguments:
- X: bfloat16 [32768, 960], P(('dp', 'fo', 'fi'))
- dY: bfloat16 [32768, 960], P(('dp', 'fo', 'fi'))
- W1: bfloat16 [960, 2560], P(None, ('fo', 'fi'))
- W3: bfloat16 [960, 2560], P(None, ('fo', 'fi'))
- W2: bfloat16 [2560, 960], P(('fo', 'fi'))
- G: float32 [8, 3, 960, 2560], P(('dp', 'fo', 'fi'))
Outputs:
- output 1: bfloat16 [32768, 960], P(('dp', 'fo', 'fi'))
- output 2: float32 [3, 960, 2560], P(None, None, ('fo', 'fi'))
- output 3: float32 [8, 3, 960, 2560], P(('dp', 'fo', 'fi'))
All inputs are finite; a program needn't handle non-finite values.
Results may differ from a plain program's by a relative error of at most 0.00912588.
Values are sent between devices in bfloat16 or wider.
A program may use at most 1 GiB of HBM per device.

v0:
```python
import jax
import jax.numpy as jnp
from jax import lax
from jax.sharding import PartitionSpec as P


def mlp_grads(x, dy, w1, w3, w2t):
    a = jnp.dot(x, w1, preferred_element_type=jnp.float32)
    b = jnp.dot(x, w3, preferred_element_type=jnp.float32)
    s = jax.nn.sigmoid(a)
    sa = a * s
    h = (sa * b).astype(jnp.bfloat16)
    dh = jnp.dot(dy, w2t, preferred_element_type=jnp.float32)
    da = (dh * b * (s * (1.0 + a * (1.0 - s)))).astype(jnp.bfloat16)
    db = (dh * sa).astype(jnp.bfloat16)
    dx = (jnp.dot(da, w1.T, preferred_element_type=jnp.float32)
          + jnp.dot(db, w3.T, preferred_element_type=jnp.float32)).astype(jnp.bfloat16)
    gw1 = jnp.dot(x.T, da, preferred_element_type=jnp.float32)
    gw3 = jnp.dot(x.T, db, preferred_element_type=jnp.float32)
    gw2 = jnp.dot(dy.T, h, preferred_element_type=jnp.float32)
    return dx, jnp.stack([gw1, gw3, gw2])


def solution(mesh):
    grp = ("fo", "fi")
    alla = ("dp", "fo", "fi")

    def local(x, dy, w1s, w3s, w2s, g):
        w1 = lax.all_gather(w1s, grp, axis=1, tiled=True)
        w3 = lax.all_gather(w3s, grp, axis=1, tiled=True)
        w2 = lax.all_gather(w2s, grp, axis=0, tiled=True)
        gs = lax.psum_scatter(g[0].astype(jnp.bfloat16), grp, scatter_dimension=2, tiled=True)
        dwn = lax.psum(gs.astype(jnp.float32), "dp")
        dx, dwl = mlp_grads(x, dy, w1, w3, w2.T)
        return dx, dwn, dwl[None]

    return jax.shard_map(
        local, mesh=mesh,
        in_specs=(P(alla, None), P(alla, None), P(None, grp), P(None, grp), P(grp, None),
                  P(alla, None, None, None)),
        out_specs=(P(alla, None), P(None, None, grp), P(alla, None, None, None)),
        check_vma=False)
```

profile of v0, /device:TPU:0, one launch (start us, length us, event | category | flops | bytes accessed | tf_op | source)
XLA Modules:
  0.0 576.3 jit_solution(2868586774576493004)
XLA Ops:
  7.2 0.0 all-gather.6.cloned.1.call-start
  7.2 0.7 all-gather.6.cloned.1.call-update
  7.9 0.0 all-gather.8.cloned.1.call-start
  7.9 0.7 all-gather.8.cloned.1.call-update
  8.6 0.0 all-gather.4.cloned.1.call-start
  8.7 0.7 all-gather.4.cloned.1.call-update
  9.4 0.0 reduce-scatter.4.cloned.1.call-start
  9.4 15.7 %convert_bitcast_fusion = bf16[3,960,2560]{2,1,0:T(8,128)(2,1)} fusion(f32[1,3,960,2560]{3,2,1,0:T(8,128)} %param.11), kind=kLoop, calls=%fused_computation.8 | loop fusion | flops 7372800 | bytes 44236800 | tf_op jit(solution)/shard_map/convert_element_type | solution.py:32
  25.1 34.0 %copy.9 = bf16[3,960,2560]{1,0,2:T(4,128)(2,1)} copy(bf16[3,960,2560]{2,1,0:T(8,128)(2,1)} %convert_bitcast_fusion) | data formatting | bytes 29491200
  59.0 42.4 %reshape.7 = bf16[2560,2880]{1,0:T(8,128)(2,1)} reshape(bf16[2560,3,960]{2,1,0:T(4,128)(2,1)} %bitcast.33) | data formatting | bytes 29491200
  101.4 0.0 reduce-scatter.4.cloned.1.call-update
  101.4 0.0 all-gather.6.cloned.1.call-done
  101.5 29.6 %fusion.5 = f32[4096,2560]{1,0:T(8,128)} fusion(bf16[4096,960]{0,1:T(8,128)(2,1)} %param.6, bf16[960,2560]{1,0:T(8,128)(2,1)} %all-gather.6.cloned.1.call-done), kind=kOutput, calls=%fused_computation.13 | convolution fusion | flops 20132659200 | bytes 54722560 | tf_op jit(solution)/shard_map/dot_general | solution.py:9
  131.1 0.0 all-gather.8.cloned.1.call-done
  131.1 29.5 %fusion.6 = f32[4096,2560]{1,0:T(8,128)} fusion(bf16[4096,960]{0,1:T(8,128)(2,1)} %param.6, bf16[960,2560]{1,0:T(8,128)(2,1)} %all-gather.8.cloned.1.call-done), kind=kOutput, calls=%fused_computation.14 | convolution fusion | flops 20132659200 | bytes 54722560 | tf_op jit(solution)/shard_map/dot_general | solution.py:8
  160.6 0.0 all-gather.4.cloned.1.call-done
  160.6 0.0 copy-start
  160.6 55.2 %multiply_convert_fusion.1 = (bf16[4096,2560]{1,0:T(8,128)(2,1)}, bf16[4096,2560]{1,0:T(8,128)(2,1)}) fusion(f32[4096,2560]{1,0:T(8,128)} %fusion.6, f32[4096,2560]{1,0:T(8,128)} %fusion.5, bf16[4096,960]{0,1:T(8,128)(2,1)} %param.7, bf16[2560,960]{0,1:T(8,128)(2,1)} %all-gather.4.cloned.1.call-done), kind=kOutput, calls=%fused_computation.1 | convolution fusion | flops 20268974080 | bytes 138608640 | tf_op jit(solution)/shard_map/dot_general | solution.py:13
  215.9 0.0 copy-done
  215.9 0.0 copy-start.1
  215.9 25.0 %convolution_bitcast_fusion = f32[1,960,2560]{2,1,0:T(8,128)} fusion(bf16[4096,960]{0,1:T(8,128)(2,1)S(1)} %copy-done, bf16[4096,2560]{1,0:T(8,128)(2,1)} %get-tuple-element.3), kind=kOutput, calls=%fused_computation.9 | convolution fusion | flops 20132659200 | bytes 38666240 | tf_op jit(solution)/shard_map/dot_general | solution.py:19
  240.9 0.0 copy-done.1
  240.9 23.0 %convolution_bitcast_fusion.1 = f32[1,960,2560]{2,1,0:T(8,128)} fusion(bf16[4096,960]{0,1:T(8,128)(2,1)S(1)} %copy-done, bf16[4096,2560]{1,0:T(8,128)(2,1)S(1)} %copy-done.1), kind=kOutput, calls=%fused_computation.10 | convolution fusion | flops 20132659200 | bytes 38666240 | tf_op jit(solution)/shard_map/dot_general | solution.py:18
  263.9 39.0 %fusion.3 = f32[1,960,2560]{2,1,0:T(8,128)} fusion(bf16[4096,960]{0,1:T(8,128)(2,1)} %param.7, f32[4096,2560]{1,0:T(8,128)} %fusion.5, f32[4096,2560]{1,0:T(8,128)} %fusion.6), kind=kOutput, calls=%fused_computation.11 | convolution fusion | flops 20195573760 | bytes 101580800 | tf_op jit(solution)/shard_map/dot_general | solution.py:20
  303.0 21.3 %maximum_bitcast_fusion = f32[1,3,960,2560]{3,2,1,0:T(8,128)} fusion(f32[1,960,2560]{2,1,0:T(8,128)} %fusion.3, f32[1,960,2560]{2,1,0:T(8,128)} %convolution_bitcast_fusion, f32[1,960,2560]{2,1,0:T(8,128)} %convolution_bitcast_fusion.1), kind=kLoop, calls=%fused_computation.5 | loop fusion | flops 14745600 | bytes 58982400 | tf_op jit(solution)/shard_map/broadcast_in_dim | solution.py:35
  324.2 25.1 %fusion.7 = f32[4096,960]{0,1:T(8,128)S(1)} fusion(bf16[4096,2560]{1,0:T(8,128)(2,1)} %get-tuple-element.4, bf16[960,2560]{1,0:T(8,128)(2,1)} %all-gather.8.cloned.1.call-done), kind=kOutput, calls=%fused_computation.15 | convolution fusion | flops 20132659200 | bytes 41615360 | tf_op jit(solution)/shard_map/dot_general | solution.py:16
  349.3 0.0 slice-done
  349.3 0.0 slice-done.1
  349.4 24.9 %add_convert_fusion = bf16[4096,960]{0,1:T(8,128)(2,1)} fusion(f32[4096,960]{0,1:T(8,128)S(1)} %fusion.7, bf16[4096,2560]{1,0:T(8,128)(2,1)} %get-tuple-element.3, bf16[960,2560]{1,0:T(8,128)(2,1)S(1)} %bitcast.36), kind=kOutput, calls=%fused_computation.7 | convolution fusion | flops 20140523520 | bytes 49479680 | tf_op jit(solution)/shard_map/dot_general | solution.py:17
  374.3 12.6 %reshape.8 = bf16[640,3,960]{2,1,0:T(4,128)(2,1)} reshape(bf16[640,2880]{1,0:T(8,128)(2,1)} %reduce-scatter.4.cloned.1.call-done) | data formatting | bytes 7372800
  386.9 8.9 %copy.10 = bf16[3,960,640]{2,1,0:T(8,128)(2,1)} copy(bf16[3,960,640]{1,0,2:T(4,128)(2,1)} %bitcast.34) | data formatting | bytes 7372800
  395.8 173.6 %all-reduce.1 = f32[3,960,640]{2,1,0:T(8,128)} all-reduce(bf16[3,960,640]{2,1,0:T(8,128)(2,1)} %copy.10), channel_id=1, replica_groups=mesh['dp'=2,'fo'=2,'fi'=2] {'dp'}, use_global_device_ids=true, to_apply=%region_1.0 | all-reduce | flops 1843200 | bytes 11059200 | tf_op jit(solution)/shard_map/psum | solution.py:33
  (4 shorter events, 0.0 us)
Async XLA Ops:
  7.2 94.3 %all-gather.6.cloned.1.call-start = ((), (), s32[]{:S(2)}) async-start(), calls=%async_computation.2 | async-start | bytes 6144000 | tf_op jit(solution)/shard_map/all_gather | solution.py:30
  7.9 123.2 %all-gather.8.cloned.1.call-start = ((), (), s32[]{:S(2)}) async-start(), calls=%async_computation.3 | async-start | bytes 6144000 | tf_op jit(solution)/shard_map/all_gather | solution.py:29
  8.6 152.0 %all-gather.4.cloned.1.call-start = ((), (), s32[]{:S(2)}) async-start(), calls=%async_computation.1 | async-start | bytes 6144000 | tf_op jit(solution)/shard_map/all_gather | solution.py:31
  9.4 364.9 %reduce-scatter.4.cloned.1.call-start = ((), (), s32[]{:S(2)}) async-start(), calls=%async_computation.4 | async-start | bytes 18841600
  160.6 55.2 %copy-start = (bf16[4096,960]{0,1:T(8,128)(2,1)S(1)}, bf16[4096,960]{0,1:T(8,128)(2,1)}, u32[]{:S(2)}) copy-start(bf16[4096,960]{0,1:T(8,128)(2,1)} %param.6) | copy-start | bytes 23592964
  215.9 25.0 %copy-start.1 = (bf16[4096,2560]{1,0:T(8,128)(2,1)S(1)}, bf16[4096,2560]{1,0:T(8,128)(2,1)}, u32[]{:S(2)}) copy-start(bf16[4096,2560]{1,0:T(8,128)(2,1)} %get-tuple-element.4) | copy-start | bytes 62914564
  303.0 46.4 %slice-start = ((s8[4915200]{0:T(1024)(128)(4,1)}), s8[4194304]{0:T(1024)(128)(4,1)S(1)}, s32[]{:S(2)}) async-start(s8[4915200]{0:T(1024)(128)(4,1)} %bitcast.35), calls=%async_computation.5 | async-start | bytes 8388608
  324.2 25.1 %slice-start.1 = ((s8[4915200]{0:T(1024)(128)(4,1)}), s8[720896]{0:T(1024)(128)(4,1)S(1)}, s32[]{:S(2)}) async-start(s8[4915200]{0:T(1024)(128)(4,1)} %bitcast.35), calls=%async_computation.6 | async-start | bytes 1441792
Sparse Core Ops, SparseCore 0:
  9.5 38.4 all-gather.5
  49.5 35.6 all-gather.7
  86.7 35.6 all-gather.3
  124.8 105.5 reduce-scatter.3
where the time goes:
time: 587 us; the launch traced here: 576 us
  matrix products  251 us (43%)
  blocking collectives  174 us (30%)
  local copies, waits for them, and re-layouts  97.9 us (17%)
  other arithmetic  36.9 us (6%)
  between operations  14.2 us (2%)
    psum x1, blocking collectives, local(): dwn = lax.psum(gs.astype(jnp.float32), 'dp')  174 us
    unnamed x12, local copies, waits for them, and re-layouts  97.9 us
    dot_general x1, matrix products, mlp_grads(): dh = jnp.dot(dy, w2t, preferred_element_type=jnp.float32)  55.2 us
    dot_general x1, matrix products, mlp_grads(): gw2 = jnp.dot(dy.T, h, preferred_element_type=jnp.float32)  39 us
    dot_general x1, matrix products, mlp_grads(): b = jnp.dot(x, w3, preferred_element_type=jnp.float32)  29.6 us
    dot_general x1, matrix products, mlp_grads(): a = jnp.dot(x, w1, preferred_element_type=jnp.float32)  29.5 us
    dot_general x1, matrix products, mlp_grads(): jnp.dot(da, w1.T, preferred_element_type=jnp.float32)  25.1 us
    dot_general x1, matrix products, mlp_grads(): gw3 = jnp.dot(x.T, db, preferred_element_type=jnp.float32)  25 us
  transfers between devices with their start and end apart: 4, of which 0 were waited for; matrix products, arithmetic and copies ran while one was open for 63% of the time, Pallas kernels for 0%

commit v1 on v0

v1 whole, which is shorter than its diff:
```python
import functools

import jax
import jax.numpy as jnp
from jax import lax
from jax.experimental import pallas as pl
from jax.experimental.pallas import tpu as pltpu
from jax.sharding import PartitionSpec as P

BF = jnp.bfloat16
F32 = jnp.float32
T, D, FF = 4096, 960, 2560
SH = FF // 4
HB = FF // 2
TB = 512
NB = 256
VM = 62 * 1024 * 1024
ANY = pl.BlockSpec(memory_space=pl.ANY)


def load_shards(c, pairs, sem):
    cps = []
    for k, (mine, other, dst) in enumerate(pairs):
        cps.append(pltpu.make_async_copy(mine, dst.at[:, pl.ds(pl.multiple_of(c * SH, 128), SH)], sem.at[2 * k]))
        cps.append(pltpu.make_async_copy(other, dst.at[:, pl.ds(pl.multiple_of((1 - c) * SH, 128), SH)], sem.at[2 * k + 1]))
    for cp in cps:
        cp.start()
    for cp in cps:
        cp.wait()


def f_kernel(s_ref, x_ref, dy_ref, w1a, w1b, w3a, w3b, w2a, w2b, h_ref, da_ref, db_ref, w1, w3, w2, xt, dyt, sem):
    @pl.when(pl.program_id(0) == 0)
    def _():
        load_shards(s_ref[0], [(w1a, w1b, w1), (w3a, w3b, w3), (w2a, w2b, w2)], sem)

    xt[...] = x_ref[...].T
    dyt[...] = dy_ref[...].T
    for n in range(HB // NB):
        cs = slice(n * NB, (n + 1) * NB)
        a = jnp.dot(xt[...], w1[:, cs], preferred_element_type=F32)
        b = jnp.dot(xt[...], w3[:, cs], preferred_element_type=F32)
        dh = jnp.dot(dyt[...], w2[:, cs], preferred_element_type=F32)
        s = jax.nn.sigmoid(a)
        sa = a * s
        h_ref[:, cs] = (sa * b).astype(BF)
        da_ref[:, cs] = (dh * b * (s * (1.0 + a * (1.0 - s)))).astype(BF)
        db_ref[:, cs] = (dh * sa).astype(BF)


def f_call(c, xT, dyT, ws):
    out = jax.ShapeDtypeStruct((T, HB), BF)
    return pl.pallas_call(
        f_kernel,
        out_shape=(out, out, out),
        grid_spec=pltpu.PrefetchScalarGridSpec(
            num_scalar_prefetch=1, grid=(T // TB,),
            in_specs=[pl.BlockSpec((D, TB), lambda i, s: (0, i))] * 2 + [ANY] * 6,
            out_specs=[pl.BlockSpec((TB, HB), lambda i, s: (i, 0))] * 3,
            scratch_shapes=[pltpu.VMEM((D, HB), BF)] * 3 + [pltpu.VMEM((TB, D), BF)] * 2
            + [pltpu.SemaphoreType.DMA((6,))]),
        compiler_params=pltpu.CompilerParams(vmem_limit_bytes=VM),
        cost_estimate=pl.CostEstimate(flops=6 * T * D * HB, bytes_accessed=4 * T * D + 6 * T * HB + 6 * D * HB,
                                      transcendentals=T * HB),
    )(c, xT, dyT, *ws)


def gw_kernel(s_ref, x_ref, dy_ref, da_ref, db_ref, h_ref, *rest):
    o_ref = rest[-1]
    m = pl.program_id(0)

    @pl.when(m == 0)
    def _():
        o_ref[0, 0] = jnp.dot(x_ref[...], da_ref[...], preferred_element_type=F32)

    @pl.when(m == 1)
    def _():
        o_ref[0, 0] = jnp.dot(x_ref[...], db_ref[...], preferred_element_type=F32)

    @pl.when(m == 2)
    def _():
        o_ref[0, 0] = jnp.dot(dy_ref[...], h_ref[...], preferred_element_type=F32)


def gw_call(half, xT, dyT, da, db, h, acc):
    nj = HB // NB
    full = pl.BlockSpec((D, T), lambda m, j, s: (0, 0))

    def col(k):
        return pl.BlockSpec((T, NB), lambda m, j, s: (0, jnp.where(m == k, j, jnp.where(m < k, 0, nj - 1))))

    args = [half, xT, dyT, da, db, h]
    specs = [full, full, col(0), col(1), col(2)]
    alias = {}
    if acc is not None:
        args.append(acc)
        specs.append(ANY)
        alias = {6: 0}
    return pl.pallas_call(
        gw_kernel,
        out_shape=jax.ShapeDtypeStruct((1, 3, D, FF), F32),
        grid_spec=pltpu.PrefetchScalarGridSpec(
            num_scalar_prefetch=1, grid=(3, nj), in_specs=specs,
            out_specs=pl.BlockSpec((1, 1, D, NB), lambda m, j, s: (0, m, 0, s[0] * nj + j))),
        input_output_aliases=alias,
        compiler_params=pltpu.CompilerParams(vmem_limit_bytes=VM),
        cost_estimate=pl.CostEstimate(flops=6 * T * D * HB, bytes_accessed=4 * T * D + 6 * T * HB + 12 * D * HB,
                                      transcendentals=0),
    )(*args)


def dx_kernel(s_ref, da0, db0, da1, db1, *rest):
    wr, (o_ref, w1o, w3o, w1n, w3n, sem) = rest[:8], rest[8:]

    @pl.when(pl.program_id(0) == 0)
    def _():
        load_shards(s_ref[0], [(wr[0], wr[1], w1o), (wr[2], wr[3], w3o), (wr[4], wr[5], w1n), (wr[6], wr[7], w3n)], sem)

    def nt(w, d):
        return lax.dot_general(w[...], d[...], (((1,), (1,)), ((), ())), preferred_element_type=F32)

    o_ref[...] = (nt(w1o, da0) + nt(w3o, db0) + nt(w1n, da1) + nt(w3n, db1)).astype(BF)


def dx_call(c, acts, ws):
    return pl.pallas_call(
        dx_kernel,
        out_shape=jax.ShapeDtypeStruct((D, T), BF),
        grid_spec=pltpu.PrefetchScalarGridSpec(
            num_scalar_prefetch=1, grid=(T // TB,),
            in_specs=[pl.BlockSpec((TB, HB), lambda i, s: (i, 0))] * 4 + [ANY] * 8,
            out_specs=pl.BlockSpec((D, TB), lambda i, s: (0, i)),
            scratch_shapes=[pltpu.VMEM((D, HB), BF)] * 4 + [pltpu.SemaphoreType.DMA((8,))]),
        compiler_params=pltpu.CompilerParams(vmem_limit_bytes=VM),
        cost_estimate=pl.CostEstimate(flops=4 * T * D * FF, bytes_accessed=4 * T * FF + 4 * D * FF + 2 * T * D,
                                      transcendentals=0),
    )(c, *acts, *ws)


RB = 240


def cast_kernel(s_ref, g_ref, a_ref, b_ref, ea_ref, eb_ref):
    o, c = s_ref[0], s_ref[1]
    for ref, oo, cc in ((a_ref, o, c), (b_ref, 1 - o, c), (ea_ref, o, 1 - c), (eb_ref, 1 - o, 1 - c)):
        ref[...] = g_ref[0, 0, :, pl.ds(pl.multiple_of((oo * 2 + cc) * SH, 128), SH)].astype(BF)


def cast_call(oc, g, m):
    out = jax.ShapeDtypeStruct((D, SH), BF)
    return pl.pallas_call(
        cast_kernel,
        out_shape=(out,) * 4,
        grid_spec=pltpu.PrefetchScalarGridSpec(
            num_scalar_prefetch=1, grid=(D // RB,),
            in_specs=[pl.BlockSpec((1, 1, RB, FF), lambda i, s: (0, m, i, 0))],
            out_specs=[pl.BlockSpec((RB, SH), lambda i, s: (i, 0))] * 4),
        compiler_params=pltpu.CompilerParams(vmem_limit_bytes=VM),
        cost_estimate=pl.CostEstimate(flops=6 * D * FF, bytes_accessed=6 * D * FF, transcendentals=0),
    )(oc, g)


def solution(mesh):
    grp = ("fo", "fi")
    alla = ("dp", "fo", "fi")
    flip = [(0, 1), (1, 0)]

    def add(*v):
        return sum(t.astype(F32) for t in v)

    def local(x, dy, w1s, w3s, w2s, g):
        o, c = lax.axis_index("fo"), lax.axis_index("fi")
        oc = jnp.stack([o, c]).astype(jnp.int32)
        cv, ov, nv = oc[1:], oc[:1], 1 - oc[:1]
        xT, dyT = x.T, dy.T
        mine = [w1s, w3s, w2s.T]
        pair = [lax.ppermute(w, "fi", flip) for w in mine]
        far = [lax.ppermute(w, "fo", flip) for w in mine]
        farp = [lax.ppermute(w, "fi", flip) for w in far]
        own = [t for p in zip(mine, pair) for t in p]
        oth = [t for p in zip(far, farp) for t in p]

        parts = [cast_call(oc, g, m) for m in range(3)]
        a_in = [lax.ppermute(p[2], "fi", flip) for p in parts]
        b_in = [lax.ppermute(p[3], "fi", flip) for p in parts]
        h0, da0, db0 = f_call(cv, xT, dyT, own)
        bs = [add(parts[m][1], b_in[m]).astype(BF) for m in range(3)]
        x_in = [lax.ppermute(t, "fo", flip) for t in bs]
        acc = gw_call(ov, xT, dyT, da0, db0, h0, None)
        h1, da1, db1 = f_call(cv, xT, dyT, oth)
        gs = [add(parts[m][0], a_in[m], x_in[m]).astype(BF) for m in range(3)]
        y_in = [lax.ppermute(t, "dp", flip) for t in gs]
        dwl = gw_call(nv, xT, dyT, da1, db1, h1, acc)
        dxT = dx_call(cv, [da0, db0, da1, db1], own[:4] + oth[:4])
        dwn = jnp.stack([add(gs[m], y_in[m]) for m in range(3)])
        return dxT.T, dwn, dwl

    return jax.shard_map(
        local, mesh=mesh,
        in_specs=(P(alla, None), P(alla, None), P(None, grp), P(None, grp), P(grp, None),
                  P(alla, None, None, None)),
        out_specs=(P(alla, None), P(None, None, grp), P(alla, None, None, None)),
        check_vma=False)
```

time: 587 us -> 342 us (0.58); the launches traced: 576 us -> 341 us
  matrix products: 251 us -> 0 us
  Pallas kernels: 0 us -> 245 us
  blocking collectives: 174 us -> 0 us
  local copies, waits for them, and re-layouts: 97.9 us -> 0.78 us
  waiting for transfers between devices: 2.1 us -> 54.7 us
  starting transfers between devices: 0.15 us -> 14 us
  between operations: 14.2 us -> 0.74 us
  other arithmetic: 36.9 us -> 26.1 us
    dot_general x8 -> x0, matrix products: 251 us -> none  [the longest x1 55.2 us: mlp_grads(): dh = jnp.dot(dy, w2t, preferred_element_type=jnp.float32)]
    pallas_call x0 -> x8, Pallas kernels: none -> 245 us  [the longest x2 87.6 us: f_call(): pl.pallas_call(f_kernel, out_shape=(out, out, out), grid_spec=pltpu.Prefe...]
    psum x1 -> x0, blocking collectives: 174 us -> none  [local(): dwn = lax.psum(gs.astype(jnp.float32), 'dp')]
    unnamed x12 -> x16, local copies, waits for them, and re-layouts: 97.9 us -> 0.78 us
    ppermute x0 -> x21, waiting for transfers between devices: none -> 54.7 us  [the longest x3 28.4 us: local(): x_in = [lax.ppermute(t, 'fo', flip) for t in bs]]
    broadcast_in_dim x1 -> x0, other arithmetic: 21.3 us -> none  [local(): return (dx, dwn, dwl[None])]
    ppermute x0 -> x21, starting transfers between devices: none -> 14 us  [the longest x3 5.39 us: local(): far = [lax.ppermute(w, 'fo', flip) for w in mine]]
    another operation x0 -> x5, other arithmetic: none -> 9.45 us  [the longest x4 8.86 us: local(): dwn = jnp.stack([add(gs[m], y_in[m]) for m in range(3)])]
  transfers between devices with their start and end apart: 4 -> 21, of which waited for: 0 -> 4; matrix products, arithmetic and copies ran while one was open for 63% -> 6% of each run, Pallas kernels for 0% -> 72%
where the time goes in v1:
time: 342 us; the launch traced here: 341 us
  Pallas kernels  245 us (72%)
  waiting for transfers between devices  54.7 us (16%)
  other arithmetic  26.1 us (8%)
  starting transfers between devices  14 us (4%)
    pallas_call x2, Pallas kernels, f_call(): pl.pallas_call(f_kernel, out_shape=(out, out, out), grid_spec=pltpu.Prefe...  87.6 us
    pallas_call x2, Pallas kernels, gw_call(): pl.pallas_call(gw_kernel, out_shape=jax.ShapeDtypeStruct((1, 3, D, FF), F...  85.7 us
    pallas_call x1, Pallas kernels, dx_call(): pl.pallas_call(dx_kernel, out_shape=jax.ShapeDtypeStruct((D, T), BF), gri...  50.5 us
    ppermute x3, waiting for transfers between devices, local(): x_in = [lax.ppermute(t, 'fo', flip) for t in bs]  28.4 us
    ppermute x3, waiting for transfers between devices, local(): far = [lax.ppermute(w, 'fo', flip) for w in mine]  26.3 us
    pallas_call x3, Pallas kernels, cast_call(): pl.pallas_call(cast_kernel, out_shape=(out,) * 4, grid_spec=pltpu.Prefetc...  21 us
    another operation x4, other arithmetic, local(): dwn = jnp.stack([add(gs[m], y_in[m]) for m in range(3)])  8.86 us
    convert_element_type x3, other arithmetic, local(): gs = [add(parts[m][0], a_in[m], x_in[m]).astype(BF) for m in range(3)]  8.61 us
  transfers between devices with their start and end apart: 21, of which 4 were waited for; matrix products, arithmetic and copies ran while one was open for 6% of the time, Pallas kernels for 72%

profile of v1, /device:TPU:0, one launch (start us, length us, event | category | flops | bytes accessed | tf_op | source)
XLA Modules:
  0.0 341.2 jit_solution(8707030459610470662)
XLA Ops:
  0.6 3.4 collective-permute-start.7
  4.0 0.6 pad_add_fusion.s_ref
  4.6 7.0 %shard_map.90 = (bf16[960,640]{1,0:T(8,128)(2,1)}, bf16[960,640]{1,0:T(8,128)(2,1)}, bf16[960,640]{1,0:T(8,128)(2,1)}, bf16[960,640]{1,0:T(8,128)(2,1)}) custom-call(s32[2]{0:T(128)} %pad_add_fusion.s_ref, f32[1,3,960,2560]{3,2,1,0:T(8,128)} %g_ref.5), custom_call_target="tpu_custom_call" | custom-call | flops 14745600 | bytes 14745600 | tf_op jit(solution)/shard_map/pallas_call | solution.py:151
  11.6 7.0 %shard_map.89 = (bf16[960,640]{1,0:T(8,128)(2,1)}, bf16[960,640]{1,0:T(8,128)(2,1)}, bf16[960,640]{1,0:T(8,128)(2,1)}, bf16[960,640]{1,0:T(8,128)(2,1)}) custom-call(s32[2]{0:T(128)} %pad_add_fusion.s_ref, f32[1,3,960,2560]{3,2,1,0:T(8,128)} %g_ref.5), custom_call_target="tpu_custom_call" | custom-call | flops 14745600 | bytes 14745600 | tf_op jit(solution)/shard_map/pallas_call | solution.py:151
  18.6 0.5 collective-permute-start.14
  19.6 7.0 %shard_map.88 = (bf16[960,640]{1,0:T(8,128)(2,1)}, bf16[960,640]{1,0:T(8,128)(2,1)}, bf16[960,640]{1,0:T(8,128)(2,1)}, bf16[960,640]{1,0:T(8,128)(2,1)}) custom-call(s32[2]{0:T(128)} %pad_add_fusion.s_ref, f32[1,3,960,2560]{3,2,1,0:T(8,128)} %g_ref.5), custom_call_target="tpu_custom_call" | custom-call | flops 14745600 | bytes 14745600 | tf_op jit(solution)/shard_map/pallas_call | solution.py:151
  26.6 4.4 %collective-permute-done.7.w2a = bf16[960,640]{1,0:T(8,128)(2,1)} collective-permute-done((bf16[960,640]{1,0:T(8,128)(2,1)}, bf16[960,640]{1,0:T(8,128)(2,1)}, u32[]{:S(2)}, u32[]{:S(2)}) %collective-permute-start.7) | collective-permute-done | bytes 1228832 | tf_op jit(solution)/shard_map/ppermute | solution.py:178
  31.0 1.7 collective-permute-start.3
  32.8 0.5 collective-permute-start.10
  33.3 2.8 add_convert_fusion.1
  36.1 2.6 add_convert_fusion.3
  39.0 21.9 %collective-permute-done.3.w1a.rest_4_ = bf16[960,640]{1,0:T(8,128)(2,1)} collective-permute-done((bf16[960,640]{1,0:T(8,128)(2,1)}, bf16[960,640]{1,0:T(8,128)(2,1)}, u32[]{:S(2)}, u32[]{:S(2)}) %collective-permute-start.3) | collective-permute-done | bytes 1228832 | tf_op jit(solution)/shard_map/ppermute | solution.py:178
  60.9 1.8 collective-permute-start.19
  63.0 0.8 copy-done.2
  63.7 43.9 %shard_map.85 = (bf16[4096,1280]{1,0:T(8,128)(2,1)}, bf16[4096,1280]{1,0:T(8,128)(2,1)}, bf16[4096,1280]{1,0:T(8,128)(2,1)}) custom-call(s32[1]{0:T(128)} %bitcast.s_ref, bf16[960,4096]{1,0:T(8,128)(2,1)} %bitcast.12, bf16[960,4096]{1,0:T(8,128)(2,1)} %bitcast.16, bf16[960,640]{1,0:T(8,128)(2,1)} %rest_0_.1, ...), custom_call_target="tpu_custom_call" | custom-call | flops 30198988800 | bytes 54558720 | tf_op jit(solution)/shard_map/pallas_call | solution.py:53
  107.6 2.6 add_convert_fusion.5
  110.4 0.8 collective-permute-start.11
  111.5 2.1 collective-permute-done.19
  113.6 26.3 %collective-permute-done.15 = bf16[960,640]{1,0:T(8,128)(2,1)} collective-permute-done((bf16[960,640]{1,0:T(8,128)(2,1)}, bf16[960,640]{1,0:T(8,128)(2,1)}, u32[]{:S(2)}, u32[]{:S(2)}) %collective-permute-start.15) | collective-permute-done | bytes 1228832 | tf_op jit(solution)/shard_map/ppermute | solution.py:188
  139.9 42.7 %shard_map.91.rest_0_ = f32[1,3,960,2560]{3,2,1,0:T(8,128)} custom-call(s32[1]{0:T(128)} %bitcast.5.s_ref, bf16[960,4096]{1,0:T(8,128)(2,1)} %bitcast.13, bf16[960,4096]{1,0:T(8,128)(2,1)} %bitcast.17, bf16[4096,1280]{1,0:T(8,128)(2,1)} %get-tuple-element.21.da0.da_ref, bf16[4096,1280]{1,0:T(8,128)(2,1)} %get-tuple-element.22.db0.db_ref, ...), custom_call_target="tpu_custom_call" | custom-call | flops 30198988800 | bytes 61931520 | tf_op jit(solution)/shard_map/pallas_call | solution.py:99
  182.7 3.2 add_convert_fusion
  185.9 2.2 add_convert_fusion.2
  188.1 1.8 collective-permute-start.20
  190.2 3.1 add_convert_fusion.4
  193.4 1.8 collective-permute-start.12
  195.1 43.7 %shard_map.86 = (bf16[4096,1280]{1,0:T(8,128)(2,1)}, bf16[4096,1280]{1,0:T(8,128)(2,1)}, bf16[4096,1280]{1,0:T(8,128)(2,1)}) custom-call(s32[1]{0:T(128)} %bitcast.s_ref, bf16[960,4096]{1,0:T(8,128)(2,1)} %bitcast.14, bf16[960,4096]{1,0:T(8,128)(2,1)} %bitcast.18, bf16[960,640]{1,0:T(8,128)(2,1)} %collective-permute-done.3.w1a.rest_4_, ...), custom_call_target="tpu_custom_call" | custom-call | flops 30198988800 | bytes 54558720 | tf_op jit(solution)/shard_map/pallas_call | solution.py:53
  238.9 50.5 %shard_map.87 = bf16[960,4096]{1,0:T(8,128)(2,1)} custom-call(s32[1]{0:T(128)} %bitcast.s_ref, bf16[4096,1280]{1,0:T(8,128)(2,1)} %get-tuple-element.21.da0.da_ref, bf16[4096,1280]{1,0:T(8,128)(2,1)} %get-tuple-element.22.db0.db_ref, bf16[4096,1280]{1,0:T(8,128)(2,1)} %get-tuple-element.23.da1.da_ref, bf16[4096,1280]{1,0:T(8,128)(2,1)} %get-tuple-element.24.db1.db_ref, ...), custom_call_target="tpu_custom_call" | custom-call | flops 40265318400 | bytes 59637760 | tf_op jit(solution)/shard_map/pallas_call | solution.py:126
  289.4 42.9 %shard_map.92 = f32[1,3,960,2560]{3,2,1,0:T(8,128)} custom-call(s32[1]{0:T(128)S(6)} %sub.3.s_ref, bf16[960,4096]{1,0:T(8,128)(2,1)} %bitcast.15, bf16[960,4096]{1,0:T(8,128)(2,1)} %bitcast.19, bf16[4096,1280]{1,0:T(8,128)(2,1)} %get-tuple-element.23.da1.da_ref, bf16[4096,1280]{1,0:T(8,128)(2,1)} %get-tuple-element.24.db1.db_ref, ...), custom_call_target="tpu_custom_call", output_to_operand_aliasing={{}: (6, {})} | custom-call | flops 30198988800 | bytes 61931520 | tf_op jit(solution)/shard_map/pallas_call | solution.py:99
  332.3 1.9 add_bitcast_fusion
  334.2 1.5 add_bitcast_fusion.1
  335.8 1.9 add_bitcast_fusion.2
  337.7 3.5 %pad_maximum_fusion = f32[3,960,640]{2,1,0:T(8,128)} fusion(f32[1,960,640]{2,1,0:T(8,128)S(1)} %add_bitcast_fusion, f32[1,960,640]{2,1,0:T(8,128)S(1)} %add_bitcast_fusion.1, f32[1,960,640]{2,1,0:T(8,128)S(1)} %add_bitcast_fusion.2), kind=kLoop, calls=%fused_computation | loop fusion | flops 3686400 | bytes 14745600 | tf_op jit(solution)/shard_map/stack | solution.py:195
  (45 shorter events, 1.8 us)
Async XLA Ops:
  0.6 30.4 %collective-permute-start.7 = (bf16[960,640]{1,0:T(8,128)(2,1)}, bf16[960,640]{1,0:T(8,128)(2,1)}, u32[]{:S(2)}, u32[]{:S(2)}) collective-permute-start(bf16[960,640]{1,0:T(8,128)(2,1)} %bitcast.20), channel_id=1, source_target_pairs={{0,2},{2,0},{1,3},{3,1},{4,6},{6,4},{5,7},{7,5}} | collective-permute-start | bytes 3686408 | tf_op jit(solution)/shard_map/ppermute | solution.py:178
  11.6 21.2 %collective-permute-start.18 = (bf16[960,640]{1,0:T(8,128)(2,1)}, bf16[960,640]{1,0:T(8,128)(2,1)}, u32[]{:S(2)}, u32[]{:S(2)}) collective-permute-start(bf16[960,640]{1,0:T(8,128)(2,1)} %get-tuple-element.36), channel_id=1, source_target_pairs={{0,1},{1,0},{2,3},{3,2},{4,5},{5,4},{6,7},{7,6}} | collective-permute-start | bytes 3686408 | tf_op jit(solution)/shard_map/ppermute | solution.py:185
  18.6 14.7 %copy-start.1 = (bf16[960,640]{1,0:T(8,128)(2,1)S(1)}, bf16[960,640]{1,0:T(8,128)(2,1)}, u32[]{:S(2)}) copy-start(bf16[960,640]{1,0:T(8,128)(2,1)} %get-tuple-element.35) | copy-start | bytes 3686404
  18.6 14.2 %collective-permute-start.14 = (bf16[960,640]{1,0:T(8,128)(2,1)}, bf16[960,640]{1,0:T(8,128)(2,1)}, u32[]{:S(2)}, u32[]{:S(2)}) collective-permute-start(bf16[960,640]{1,0:T(8,128)(2,1)} %get-tuple-element.32), channel_id=1, source_target_pairs={{0,1},{1,0},{2,3},{3,2},{4,5},{5,4},{6,7},{7,6}} | collective-permute-start | bytes 3686408 | tf_op jit(solution)/shard_map/ppermute | solution.py:185
  19.1 19.6 %collective-permute-start.2 = (bf16[960,640]{1,0:T(8,128)(2,1)}, bf16[960,640]{1,0:T(8,128)(2,1)}, u32[]{:S(2)}, u32[]{:S(2)}) collective-permute-start(bf16[960,640]{1,0:T(8,128)(2,1)} %bitcast.21), channel_id=1, source_target_pairs={{0,1},{1,0},{2,3},{3,2},{4,5},{5,4},{6,7},{7,6}} | collective-permute-start | bytes 3686408 | tf_op jit(solution)/shard_map/ppermute | solution.py:177
  19.1 19.9 %collective-permute-start = (bf16[960,640]{1,0:T(8,128)(2,1)}, bf16[960,640]{1,0:T(8,128)(2,1)}, u32[]{:S(2)}, u32[]{:S(2)}) collective-permute-start(bf16[960,640]{1,0:T(8,128)(2,1)} %rest_0_.1), channel_id=1, source_target_pairs={{0,1},{1,0},{2,3},{3,2},{4,5},{5,4},{6,7},{7,6}} | collective-permute-start | bytes 3686408 | tf_op jit(solution)/shard_map/ppermute | solution.py:177
  31.0 29.9 %collective-permute-start.3 = (bf16[960,640]{1,0:T(8,128)(2,1)}, bf16[960,640]{1,0:T(8,128)(2,1)}, u32[]{:S(2)}, u32[]{:S(2)}) collective-permute-start(bf16[960,640]{1,0:T(8,128)(2,1)} %rest_0_.1), channel_id=1, source_target_pairs={{0,2},{2,0},{1,3},{3,1},{4,6},{6,4},{5,7},{7,5}} | collective-permute-start | bytes 3686408 | tf_op jit(solution)/shard_map/ppermute | solution.py:178
  32.8 28.2 %collective-permute-start.1 = (bf16[960,640]{1,0:T(8,128)(2,1)}, bf16[960,640]{1,0:T(8,128)(2,1)S(1)}, u32[]{:S(2)}, u32[]{:S(2)}) collective-permute-start(bf16[960,640]{1,0:T(8,128)(2,1)} %rest_2_.1), channel_id=1, source_target_pairs={{0,1},{1,0},{2,3},{3,2},{4,5},{5,4},{6,7},{7,6}} | collective-permute-start | bytes 3686408 | tf_op jit(solution)/shard_map/ppermute | solution.py:177
  32.8 29.9 %collective-permute-start.10 = (bf16[960,640]{1,0:T(8,128)(2,1)}, bf16[960,640]{1,0:T(8,128)(2,1)S(1)}, u32[]{:S(2)}, u32[]{:S(2)}) collective-permute-start(bf16[960,640]{1,0:T(8,128)(2,1)} %get-tuple-element.28), channel_id=1, source_target_pairs={{0,1},{1,0},{2,3},{3,2},{4,5},{5,4},{6,7},{7,6}} | collective-permute-start | bytes 3686408 | tf_op jit(solution)/shard_map/ppermute | solution.py:185
  33.3 2.8 copy-start.3
  38.7 71.5 %collective-permute-start.5 = (bf16[960,640]{1,0:T(8,128)(2,1)}, bf16[960,640]{1,0:T(8,128)(2,1)}, u32[]{:S(2)}, u32[]{:S(2)}) collective-permute-start(bf16[960,640]{1,0:T(8,128)(2,1)} %rest_2_.1), channel_id=1, source_target_pairs={{0,2},{2,0},{1,3},{3,1},{4,6},{6,4},{5,7},{7,5}} | collective-permute-start | bytes 3686408 | tf_op jit(solution)/shard_map/ppermute | solution.py:178
  39.0 71.4 %collective-permute-start.17 = (bf16[960,640]{1,0:T(8,128)(2,1)}, bf16[960,640]{1,0:T(8,128)(2,1)}, u32[]{:S(2)}, u32[]{:S(2)}) collective-permute-start(bf16[960,640]{1,0:T(8,128)(2,1)} %get-tuple-element.34), channel_id=1, source_target_pairs={{0,1},{1,0},{2,3},{3,2},{4,5},{5,4},{6,7},{7,6}} | collective-permute-start | bytes 3686408 | tf_op jit(solution)/shard_map/ppermute | solution.py:184
  60.9 50.3 %collective-permute-start.13 = (bf16[960,640]{1,0:T(8,128)(2,1)}, bf16[960,640]{1,0:T(8,128)(2,1)}, u32[]{:S(2)}, u32[]{:S(2)}) collective-permute-start(bf16[960,640]{1,0:T(8,128)(2,1)} %get-tuple-element.30), channel_id=1, source_target_pairs={{0,1},{1,0},{2,3},{3,2},{4,5},{5,4},{6,7},{7,6}} | collective-permute-start | bytes 3686408 | tf_op jit(solution)/shard_map/ppermute | solution.py:184
  60.9 2.1 copy-start.7
  60.9 52.7 %collective-permute-start.19 = (bf16[960,640]{1,0:T(8,128)(2,1)}, bf16[960,640]{1,0:T(8,128)(2,1)}, u32[]{:S(2)}, u32[]{:S(2)}) collective-permute-start(bf16[960,640]{1,0:T(8,128)(2,1)} %add_convert_fusion.1), channel_id=1, source_target_pairs={{0,2},{2,0},{1,3},{3,1},{4,6},{6,4},{5,7},{7,5}} | collective-permute-start | bytes 3686408 | tf_op jit(solution)/shard_map/ppermute | solution.py:188
  62.7 1.0 copy-start.2
  62.7 77.2 %collective-permute-start.15 = (bf16[960,640]{1,0:T(8,128)(2,1)}, bf16[960,640]{1,0:T(8,128)(2,1)}, u32[]{:S(2)}, u32[]{:S(2)}) collective-permute-start(bf16[960,640]{1,0:T(8,128)(2,1)} %add_convert_fusion.3), channel_id=1, source_target_pairs={{0,2},{2,0},{1,3},{3,1},{4,6},{6,4},{5,7},{7,5}} | collective-permute-start | bytes 3686408 | tf_op jit(solution)/shard_map/ppermute | solution.py:188
  63.7 43.9 %copy-start = (bf16[960,640]{1,0:T(8,128)(2,1)S(1)}, bf16[960,640]{1,0:T(8,128)(2,1)}, u32[]{:S(2)}) copy-start(bf16[960,640]{1,0:T(8,128)(2,1)} %get-tuple-element.27) | copy-start | bytes 3686404
  110.2 77.9 %collective-permute-start.9 = (bf16[960,640]{1,0:T(8,128)(2,1)}, bf16[960,640]{1,0:T(8,128)(2,1)}, u32[]{:S(2)}, u32[]{:S(2)}) collective-permute-start(bf16[960,640]{1,0:T(8,128)(2,1)} %get-tuple-element.26), channel_id=1, source_target_pairs={{0,1},{1,0},{2,3},{3,2},{4,5},{5,4},{6,7},{7,6}} | collective-permute-start | bytes 3686408 | tf_op jit(solution)/shard_map/ppermute | solution.py:184
  110.4 79.5 %collective-permute-start.11 = (bf16[960,640]{1,0:T(8,128)(2,1)}, bf16[960,640]{1,0:T(8,128)(2,1)}, u32[]{:S(2)}, u32[]{:S(2)}) collective-permute-start(bf16[960,640]{1,0:T(8,128)(2,1)} %add_convert_fusion.5), channel_id=1, source_target_pairs={{0,2},{2,0},{1,3},{3,1},{4,6},{6,4},{5,7},{7,5}} | collective-permute-start | bytes 3686408 | tf_op jit(solution)/shard_map/ppermute | solution.py:188
  111.3 82.1 %collective-permute-start.8 = (bf16[960,640]{1,0:T(8,128)(2,1)}, bf16[960,640]{1,0:T(8,128)(2,1)}, u32[]{:S(2)}, u32[]{:S(2)}) collective-permute-start(bf16[960,640]{1,0:T(8,128)(2,1)} %collective-permute-done.7.w2a), channel_id=1, source_target_pairs={{0,1},{1,0},{2,3},{3,2},{4,5},{5,4},{6,7},{7,6}} | collective-permute-start | bytes 3686408 | tf_op jit(solution)/shard_map/ppermute | solution.py:179
  113.6 81.5 %collective-permute-start.4 = (bf16[960,640]{1,0:T(8,128)(2,1)}, bf16[960,640]{1,0:T(8,128)(2,1)}, u32[]{:S(2)}, u32[]{:S(2)}) collective-permute-start(bf16[960,640]{1,0:T(8,128)(2,1)} %collective-permute-done.3.w1a.rest_4_), channel_id=1, source_target_pairs={{0,1},{1,0},{2,3},{3,2},{4,5},{5,4},{6,7},{7,6}} | collective-permute-start | bytes 3686408 | tf_op jit(solution)/shard_map/ppermute | solution.py:179
  139.9 55.2 %collective-permute-start.6 = (bf16[960,640]{1,0:T(8,128)(2,1)}, bf16[960,640]{1,0:T(8,128)(2,1)}, u32[]{:S(2)}, u32[]{:S(2)}) collective-permute-start(bf16[960,640]{1,0:T(8,128)(2,1)} %collective-permute-done.5.w3a.rest_6_), channel_id=1, source_target_pairs={{0,1},{1,0},{2,3},{3,2},{4,5},{5,4},{6,7},{7,6}} | collective-permute-start | bytes 3686408 | tf_op jit(solution)/shard_map/ppermute | solution.py:179
  139.9 42.7 %copy-start.4 = (bf16[960,640]{1,0:T(8,128)(2,1)S(1)}, bf16[960,640]{1,0:T(8,128)(2,1)}, u32[]{:S(2)}) copy-start(bf16[960,640]{1,0:T(8,128)(2,1)} %get-tuple-element.33) | copy-start | bytes 3686404
  182.7 3.2 copy-start.6
  185.9 4.3 %copy-start.5 = (bf16[960,640]{1,0:T(8,128)(2,1)S(1)}, bf16[960,640]{1,0:T(8,128)(2,1)}, u32[]{:S(2)}) copy-start(bf16[960,640]{1,0:T(8,128)(2,1)} %get-tuple-element.25) | copy-start | bytes 3686404
  188.1 144.2 %collective-permute-start.20 = (bf16[960,640]{1,0:T(8,128)(2,1)}, bf16[960,640]{1,0:T(8,128)(2,1)}, u32[]{:S(2)}, u32[]{:S(2)}) collective-permute-start(bf16[960,640]{1,0:T(8,128)(2,1)} %add_convert_fusion), channel_id=1, source_target_pairs={{0,4},{4,0},{1,5},{5,1},{2,6},{6,2},{3,7},{7,3}} | collective-permute-start | bytes 3686408 | tf_op jit(solution)/shard_map/ppermute | solution.py:192
  189.9 144.3 %collective-permute-start.16 = (bf16[960,640]{1,0:T(8,128)(2,1)S(1)}, bf16[960,640]{1,0:T(8,128)(2,1)}, u32[]{:S(2)}, u32[]{:S(2)}) collective-permute-start(bf16[960,640]{1,0:T(8,128)(2,1)S(1)} %add_convert_fusion.2), channel_id=1, source_target_pairs={{0,4},{4,0},{1,5},{5,1},{2,6},{6,2},{3,7},{7,3}} | collective-permute-start | bytes 3686408 | tf_op jit(solution)/shard_map/ppermute | solution.py:192
  193.4 142.4 %collective-permute-start.12 = (bf16[960,640]{1,0:T(8,128)(2,1)}, bf16[960,640]{1,0:T(8,128)(2,1)}, u32[]{:S(2)}, u32[]{:S(2)}) collective-permute-start(bf16[960,640]{1,0:T(8,128)(2,1)} %add_convert_fusion.4), channel_id=1, source_target_pairs={{0,4},{4,0},{1,5},{5,1},{2,6},{6,2},{3,7},{7,3}} | collective-permute-start | bytes 3686408 | tf_op jit(solution)/shard_map/ppermute | solution.py:192

commit v2 on v0

v2 whole, which is shorter than its diff:
```python
import jax
import jax.numpy as jnp
from jax import lax
from jax.experimental import pallas as pl
from jax.experimental.pallas import tpu as pltpu
from jax.sharding import PartitionSpec as P

BF = jnp.bfloat16
F32 = jnp.float32
T, D, FF = 4096, 960, 2560
SH = FF // 4
HB = FF // 2
TB = 512
NT = T // TB
NB = 256
RC = 240
NK = 3 * D // RC
DH = D // 2
VM = 63 * 1024 * 1024
ANY = pl.BlockSpec(memory_space=pl.ANY)
DMA = pltpu.SemaphoreType.DMA


def rcopy(src, dst, ss, rs, dev):
    return pltpu.make_async_remote_copy(src_ref=src, dst_ref=dst, send_sem=ss, recv_sem=rs,
                                        device_id=dev, device_id_type=pl.DeviceIdType.MESH)


def main_kernel(x, dy, w1s, w3s, w2s, g,
                h, da, db, dxp, dx, rn, ra, gs,
                wo, wn, xb, yb, xt, yt, hb, dab, dbb, pb, ob, xs, xr, nb, ab, gb,
                wl, wcs, wcr, wxs, wxr, wys, wyr, w1fs, w1fr, w2fs, w2fr,
                gns, gnr, gas, gar, xss, xsr, ldn, lda, gst, xsem, hsem, psem, osem):
    d, o, c = lax.axis_index("dp"), lax.axis_index("fo"), lax.axis_index("fi")
    cdev, xdev, ydev = (d, o, 1 - c), (d, 1 - o, c), (1 - d, o, c)
    shards = (w1s, w3s, w2s)

    def cols(cc):
        return pl.ds(pl.multiple_of(cc * SH, 128), SH)

    def gcols(oo, cc):
        return pl.ds(pl.multiple_of((oo * 2 + cc) * SH, 128), SH)

    def rows(k):
        return pl.ds(pl.multiple_of(k * RC, 16), RC)

    def half(dd):
        return pl.ds(pl.multiple_of(dd * DH, 16), DH)

    bar = pltpu.get_barrier_semaphore()
    for dev in (cdev, xdev, ydev):
        pl.semaphore_signal(bar, inc=1, device_id=dev, device_id_type=pl.DeviceIdType.MESH)
    pl.semaphore_wait(bar, 3)

    def c_own(m):
        return rcopy(shards[m], wo.at[m, :, cols(c)], wcs.at[m], wcr.at[m], cdev)

    def x_own(m):
        return rcopy(shards[m].at[half(d), :], wn.at[m, half(d), cols(c)], wxs.at[m], wxr.at[m], xdev)

    def y_fwd(m):
        v = wn.at[m, half(d), cols(c)]
        return rcopy(v, v, wys.at[m], wyr.at[m], ydev)

    def c_fwd1(m):
        v = wn.at[m, half(d), cols(c)]
        return rcopy(v, v, w1fs.at[m], w1fr.at[m], cdev)

    def c_fwd2(m):
        v = wn.at[m, half(1 - d), cols(c)]
        return rcopy(v, v, w2fs.at[m], w2fr.at[m], cdev)

    def l_own(m):
        return pltpu.make_async_copy(shards[m], wo.at[m, :, cols(c)], wl.at[m])

    def g_n(k):
        return rcopy(g.at[rows(k), gcols(1 - o, 1 - c)], rn.at[rows(k), :], gns.at[k], gnr.at[k], cdev)

    def g_a(k):
        return rcopy(g.at[rows(k), gcols(o, 1 - c)], ra.at[rows(k), :], gas.at[k], gar.at[k], cdev)

    def x_sum(k):
        return rcopy(xs.at[k], xr.at[k], xss.at[k], xsr.at[k], xdev)

    def loads(k, oo, rec, buf, sem):
        q = k % 2
        return (pltpu.make_async_copy(g.at[rows(k), gcols(oo, c)], buf.at[q, 0], sem.at[q, 0]),
                pltpu.make_async_copy(rec.at[rows(k), :], buf.at[q, 1], sem.at[q, 1]))

    def load_n(k):
        return loads(k, 1 - o, rn, nb, ldn)

    def load_a(k):
        return loads(k, o, ra, ab, lda)

    def start_n(k):
        g_n(k).wait_recv()
        for cp in load_n(k):
            cp.start()

    def start_a(k):
        g_a(k).wait_recv()
        for cp in load_a(k):
            cp.start()

    def g_out(k):
        return pltpu.make_async_copy(gb.at[k % 2], gs.at[rows(k), :], gst.at[k % 2])

    def pair_sum(buf, q):
        return buf[q, 0].astype(BF).astype(F32) + buf[q, 1].astype(BF).astype(F32)

    def sum1(k):
        for cp in load_n(k):
            cp.wait()
        xs[k] = pair_sum(nb, k % 2).astype(BF)
        x_sum(k).start()

    def sum2(k):
        for cp in load_a(k):
            cp.wait()
        x_sum(k).wait_recv()
        gb[k % 2] = (pair_sum(ab, k % 2) + xr[k].astype(F32)).astype(BF)
        g_out(k).start()

    def tiles(j):
        q = j % 2
        t = pl.ds(pl.multiple_of((j % NT) * TB, 128), TB)
        return (pltpu.make_async_copy(x.at[:, t], xb.at[q], xsem.at[q, 0]),
                pltpu.make_async_copy(dy.at[:, t], yb.at[q], xsem.at[q, 1]))

    def acts(j):
        q = j % 2
        t = pl.ds(pl.multiple_of(j * TB, 128), TB)
        return (pltpu.make_async_copy(hb.at[q], h.at[t, :], hsem.at[q, 0]),
                pltpu.make_async_copy(dab.at[q], da.at[t, :], hsem.at[q, 1]),
                pltpu.make_async_copy(dbb.at[q], db.at[t, :], hsem.at[q, 2]))

    def tok(i):
        return pl.ds(pl.multiple_of(i * TB, 128), TB)

    def p_out(i):
        return pltpu.make_async_copy(pb.at[i % 2], dxp.at[:, tok(i)], psem.at[0, i % 2])

    def p_in(i):
        return pltpu.make_async_copy(dxp.at[:, tok(i)], pb.at[i % 2], psem.at[1, i % 2])

    def d_out(i):
        return pltpu.make_async_copy(ob.at[i % 2], dx.at[:, tok(i)], osem.at[i % 2])

    for m in range(3):
        l_own(m).start()
        c_own(m).start()
    for m in range(3):
        x_own(m).start()
    for cp in tiles(0):
        cp.start()

    @pl.loop(0, NK)
    def _(k):
        g_n(k).start()

    @pl.loop(0, NK)
    def _(k):
        g_a(k).start()

    for m in range(3):
        l_own(m).wait()
        c_own(m).wait_recv()

    def step(p, i):
        j = p * NT + i
        q = j % 2
        w = (wo, wn)[p]
        for cp in tiles(j):
            cp.wait()

        @pl.when(j < 2 * NT - 1)
        def _():
            for cp in tiles(j + 1):
                cp.start()

        if p == 0:
            for m, (s1, s2) in enumerate(((2, 4), (3, 6), (5, 8))):
                @pl.when(j == s1)
                def _():
                    y = x_own(m)
                    y.wait_recv()
                    y_fwd(m).start()
                    c_fwd1(m).start()

                if s2 < 8:
                    @pl.when(j == s2)
                    def _():
                        y_fwd(m).wait_recv()
                        c_fwd2(m).start()
        else:
            @pl.when(i < NT - 1)
            def _():
                p_in(i + 1).start()

        @pl.when((j >= 1) & (j < 1 + NK))
        def _():
            start_n(j - 1)

        @pl.when((j >= 2) & (j < 2 + NK))
        def _():
            sum1(j - 2)

        @pl.when(j >= 5)
        def _():
            start_a(j - 5)

        @pl.when(j >= 8)
        def _():
            g_out(j - 8).wait()

        @pl.when(j >= 6)
        def _():
            sum2(j - 6)

        def free():
            for cp in acts(j - 2):
                cp.wait()

        if p == 0:
            pl.when(i >= 2)(free)
        else:
            free()
        xt[...] = xb[q].T
        yt[...] = yb[q].T
        for n in range(HB // NB):
            cs = slice(n * NB, (n + 1) * NB)
            a = jnp.dot(xt[...], w[0, :, cs], preferred_element_type=F32)
            b = jnp.dot(xt[...], w[1, :, cs], preferred_element_type=F32)
            dh = jnp.dot(yt[...], w[2, :, cs], preferred_element_type=F32)
            s = jax.nn.sigmoid(a)
            sa = a * s
            hb[q, :, cs] = (sa * b).astype(BF)
            dab[q, :, cs] = (dh * b * (s * (1.0 + a * (1.0 - s)))).astype(BF)
            dbb[q, :, cs] = (dh * sa).astype(BF)
        for cp in acts(j):
            cp.start()

        def nt(m, v):
            return lax.dot_general(w[m], v[q], (((1,), (1,)), ((), ())), preferred_element_type=F32)

        if p == 0:
            @pl.when(i >= 2)
            def _():
                p_out(i - 2).wait()
            pb[q] = nt(0, dab) + nt(1, dbb)
            p_out(i).start()
        else:
            p_in(i).wait()

            @pl.when(i >= 2)
            def _():
                d_out(i - 2).wait()
            ob[q] = (pb[q] + nt(0, dab) + nt(1, dbb)).astype(BF)
            d_out(i).start()

    @pl.loop(0, NT)
    def _(i):
        step(0, i)

    for i in (NT - 2, NT - 1):
        p_out(i).wait()
    p_in(0).start()
    y_fwd(2).wait_recv()
    c_fwd2(2).start()
    for m in range(3):
        c_fwd1(m).wait_recv()
        c_fwd2(m).wait_recv()

    @pl.loop(0, NT)
    def _(i):
        step(1, i)

    start_a(NK - 1)
    for k in (NK - 2, NK - 1):
        g_out(k - 2).wait()
        sum2(k)
    for k in (NK - 2, NK - 1):
        g_out(k).wait()
    for i in (NT - 2, NT - 1):
        d_out(i).wait()
        for cp in acts(NT + i):
            cp.wait()
    for m in range(3):
        for f in (c_own, x_own, y_fwd, c_fwd1, c_fwd2):
            f(m).wait_send()

    @pl.loop(0, NK)
    def _(k):
        g_n(k).wait_send()
        g_a(k).wait_send()
        x_sum(k).wait_send()


def main_call(xT, dyT, w1s, w3s, w2sT, g2):
    act = jax.ShapeDtypeStruct((2 * T, HB), BF)
    outs = (act, act, act, jax.ShapeDtypeStruct((D, T), F32), jax.ShapeDtypeStruct((D, T), BF),
            jax.ShapeDtypeStruct((3 * D, SH), F32), jax.ShapeDtypeStruct((3 * D, SH), F32),
            jax.ShapeDtypeStruct((3 * D, SH), BF))
    V = pltpu.VMEM
    return pl.pallas_call(
        main_kernel,
        out_shape=outs,
        in_specs=[ANY] * 6,
        out_specs=(ANY,) * 8,
        scratch_shapes=[
            V((3, D, HB), BF), V((3, D, HB), BF),
            V((2, D, TB), BF), V((2, D, TB), BF), V((TB, D), BF), V((TB, D), BF),
            V((2, TB, HB), BF), V((2, TB, HB), BF), V((2, TB, HB), BF),
            V((2, D, TB), F32), V((2, D, TB), BF),
            V((NK, RC, SH), BF), V((NK, RC, SH), BF),
            V((2, 2, RC, SH), F32), V((2, 2, RC, SH), F32), V((2, RC, SH), BF),
        ] + [DMA((3,))] * 11 + [DMA((NK,))] * 6
        + [DMA((2, 2)), DMA((2, 2)), DMA((2,)), DMA((2, 2)), DMA((2, 3)), DMA((2, 2)), DMA((2,))],
        compiler_params=pltpu.CompilerParams(vmem_limit_bytes=VM, collective_id=0, has_side_effects=True),
        cost_estimate=pl.CostEstimate(flops=10 * T * D * FF, bytes_accessed=200_000_000, transcendentals=T * FF),
    )(xT, dyT, w1s, w3s, w2sT, g2)


def gw_kernel(s_ref, x_ref, dy_ref, da_ref, db_ref, h_ref, o_ref, xv, yv, sem):
    m, p, j = pl.program_id(0), pl.program_id(1), pl.program_id(2)
    cx = pltpu.make_async_copy(x_ref, xv, sem.at[0])
    cy = pltpu.make_async_copy(dy_ref, yv, sem.at[1])

    @pl.when((m == 0) & (p == 0) & (j == 0))
    def _():
        cx.start()
        cy.start()
        cx.wait()

    @pl.when((m == 2) & (p == 0) & (j == 0))
    def _():
        cy.wait()

    for k, (lhs, rhs) in enumerate(((xv, da_ref), (xv, db_ref), (yv, h_ref))):
        @pl.when(m == k)
        def _():
            o_ref[0, 0] = jnp.dot(lhs[...], rhs[...], preferred_element_type=F32)


def gw_call(ov, xT, dyT, da, db, h):
    nj = HB // NB

    def col(k):
        return pl.BlockSpec((T, NB), lambda m, p, j, s: (
            jnp.where(m == k, p, jnp.where(m < k, 0, 1)), jnp.where(m == k, j, jnp.where(m < k, 0, nj - 1))))

    return pl.pallas_call(
        gw_kernel,
        out_shape=jax.ShapeDtypeStruct((1, 3, D, FF), F32),
        grid_spec=pltpu.PrefetchScalarGridSpec(
            num_scalar_prefetch=1, grid=(3, 2, nj), in_specs=[ANY, ANY, col(0), col(1), col(2)],
            out_specs=pl.BlockSpec((1, 1, D, NB), lambda m, p, j, s: (0, m, 0, jnp.where(p == 0, s[0], 1 - s[0]) * nj + j)),
            scratch_shapes=[pltpu.VMEM((D, T), BF)] * 2 + [DMA((2,))]),
        compiler_params=pltpu.CompilerParams(vmem_limit_bytes=VM),
        cost_estimate=pl.CostEstimate(flops=6 * T * D * FF, bytes_accessed=4 * T * D + 6 * T * FF + 12 * D * FF,
                                      transcendentals=0),
    )(ov, xT, dyT, da, db, h)


def final_kernel(g_ref, y_ref, o_ref):
    o_ref[...] = g_ref[...].astype(F32) + y_ref[...].astype(F32)


def final_call(gs, ys):
    rb = 480
    spec = pl.BlockSpec((rb, SH), lambda i: (i, 0))
    return pl.pallas_call(
        final_kernel,
        out_shape=jax.ShapeDtypeStruct((3 * D, SH), F32),
        grid=(3 * D // rb,), in_specs=[spec, spec], out_specs=spec,
        compiler_params=pltpu.CompilerParams(vmem_limit_bytes=16 * 1024 * 1024),
        cost_estimate=pl.CostEstimate(flops=3 * D * SH, bytes_accessed=24 * D * SH, transcendentals=0),
    )(gs, ys)


def solution(mesh):
    grp = ("fo", "fi")
    alla = ("dp", "fo", "fi")
    flip = [(0, 1), (1, 0)]

    def local(x, dy, w1s, w3s, w2s, g):
        ov = lax.axis_index("fo").astype(jnp.int32).reshape(1)
        xT, dyT = x.T, dy.T
        h, da, db, _, dxT, _, _, gs = main_call(xT, dyT, w1s, w3s, w2s.T, g.reshape(3 * D, FF))
        ys = lax.ppermute(gs, "dp", flip)
        dwl = gw_call(ov, xT, dyT, da, db, h)
        ys, dwl = lax.optimization_barrier((ys, dwl))
        dwn = final_call(gs, ys).reshape(3, D, SH)
        return dxT.T, dwn, dwl

    return jax.shard_map(
        local, mesh=mesh,
        in_specs=(P(alla, None), P(alla, None), P(None, grp), P(None, grp), P(grp, None),
                  P(alla, None, None, None)),
        out_specs=(P(alla, None), P(None, None, grp), P(alla, None, None, None)),
        check_vma=False)
```

time: 587 us -> 240 us (0.41); the launches traced: 576 us -> 240 us
  matrix products: 251 us -> 0 us
  Pallas kernels: 0 us -> 229 us
  blocking collectives: 174 us -> 0 us
  local copies, waits for them, and re-layouts: 97.9 us -> 5.27 us
  other arithmetic: 36.9 us -> 0 us
  between operations: 14.2 us -> 0.65 us
    dot_general x8 -> x0, matrix products: 251 us -> none  [the longest x1 55.2 us: mlp_grads(): dh = jnp.dot(dy, w2t, preferred_element_type=jnp.float32)]
    pallas_call x0 -> x3, Pallas kernels: none -> 229 us  [the longest x1 145 us: main_call(): pl.pallas_call(main_kernel, out_shape=outs, in_specs=[ANY] * 6, out_specs...]
    psum x1 -> x0, blocking collectives: 174 us -> none  [local(): dwn = lax.psum(gs.astype(jnp.float32), 'dp')]
    unnamed x12 -> x5, local copies, waits for them, and re-layouts: 97.9 us -> 5.27 us
    broadcast_in_dim x1 -> x0, other arithmetic: 21.3 us -> none  [local(): return (dx, dwn, dwl[None])]
    convert_element_type x1 -> x0, other arithmetic: 15.7 us -> none  [local(): g[0].astype(jnp.bfloat16)]
  transfers between devices with their start and end apart: 4 -> 1, of which waited for: 0 -> 1; matrix products, arithmetic and copies ran while one was open for 63% -> 0% of each run, Pallas kernels for 0% -> 32%
where the time goes in v2:
time: 240 us
  Pallas kernels  229 us (95%)
  local copies, waits for them, and re-layouts  5.27 us (2%)
  waiting for transfers between devices  3.04 us (1%)
    pallas_call x1, Pallas kernels, main_call(): pl.pallas_call(main_kernel, out_shape=outs, in_specs=[ANY] * 6, out_specs...  145 us
    pallas_call x1, Pallas kernels, gw_call(): pl.pallas_call(gw_kernel, out_shape=jax.ShapeDtypeStruct((1, 3, D, FF), F...  76.7 us
    pallas_call x1, Pallas kernels, final_call(): pl.pallas_call(final_kernel, out_shape=jax.ShapeDtypeStruct((3 * D, SH),...  7.39 us
    unnamed x5, local copies, waits for them, and re-layouts  5.27 us
  transfers between devices with their start and end apart: 1, of which 1 were waited for; matrix products, arithmetic and copies ran while one was open for 0% of the time, Pallas kernels for 32%

profile of v2, /device:TPU:0, one launch (start us, length us, event | category | flops | bytes accessed | tf_op | source)
XLA Modules:
  0.0 239.9 jit_solution(103773527792730717)
XLA Ops:
  0.6 145.3 %shard_map.85 = (bf16[8192,1280]{1,0:T(8,128)(2,1)}, bf16[8192,1280]{1,0:T(8,128)(2,1)}, bf16[8192,1280]{1,0:T(8,128)(2,1)}, f32[960,4096]{1,0:T(8,128)}, bf16[9...) custom-call(bf16[960,4096]{1,0:T(8,128)(2,1)} %bitcast.10, ...), custom_call_target="tpu_custom_call" | custom-call | flops 100663296000 | bytes 200000000 | tf_op jit(solution)/shard_map/pallas_call | solution.py:306
  146.0 1.5 collective-permute-start
  147.5 76.7 %shard_map.86 = f32[1,3,960,2560]{3,2,1,0:T(8,128)} custom-call(s32[1]{0:T(128)} %bitcast.5.s_ref, bf16[960,4096]{1,0:T(8,128)(2,1)} %bitcast.11, bf16[960,4096]{1,0:T(8,128)(2,1)} %bitcast.13, bf16[8192,1280]{1,0:T(8,128)(2,1)} %get-tuple-element.12.da_ref, bf16[8192,1280]{1,0:T(8,128)(2,1)} %get-tuple-element.13.db_ref, ...), custom_call_target="tpu_custom_call" | custom-call | flops 60397977600 | bytes 108134400 | tf_op jit(solution)/shard_map/pallas_call | solution.py:353
  224.2 3.0 %collective-permute-done.y_ref = bf16[2880,640]{1,0:T(8,128)(2,1)} collective-permute-done((bf16[2880,640]{1,0:T(8,128)(2,1)}, bf16[2880,640]{1,0:T(8,128)(2,1)}, u32[]{:S(2)}, u32[]{:S(2)}) %collective-permute-start) | collective-permute-done | bytes 3686432 | tf_op jit(solution)/shard_map/ppermute | solution.py:391
  227.2 0.0 copy-start
  227.2 2.0 copy-done
  229.3 0.0 copy-start.1
  229.3 7.4 %shard_map.87 = f32[2880,640]{1,0:T(8,128)} custom-call(bf16[2880,640]{1,0:T(8,128)(2,1)S(1)} %copy-done, bf16[2880,640]{1,0:T(8,128)(2,1)} %collective-permute-done.y_ref), custom_call_target="tpu_custom_call" | custom-call | flops 1843200 | bytes 14745600 | tf_op jit(solution)/shard_map/pallas_call | solution.py:373
  236.7 0.0 copy-done.1
  236.7 3.2 %copy.10 = bf16[4096,960]{0,1:T(8,128)(2,1)} copy(bf16[4096,960]{0,1:T(8,128)(2,1)S(1)} %bitcast.7) | data formatting | bytes 15728640
Async XLA Ops:
  146.0 81.3 %collective-permute-start = (bf16[2880,640]{1,0:T(8,128)(2,1)}, bf16[2880,640]{1,0:T(8,128)(2,1)}, u32[]{:S(2)}, u32[]{:S(2)}) collective-permute-start(bf16[2880,640]{1,0:T(8,128)(2,1)} %get-tuple-element.11.g_ref), channel_id=1, source_target_pairs={{0,4},{4,0},{1,5},{5,1},{2,6},{6,2},{3,7},{7,3}} | collective-permute-start | bytes 11059208 | tf_op jit(solution)/shard_map/ppermute | solution.py:391
  227.2 2.0 copy-start
  229.3 7.4 %copy-start.1 = (bf16[960,4096]{1,0:T(8,128)(2,1)S(1)}, bf16[960,4096]{1,0:T(8,128)(2,1)}, u32[]{:S(2)}) copy-start(bf16[960,4096]{1,0:T(8,128)(2,1)} %get-tuple-element.10) | copy-start | bytes 23592964

commit v3 on v2

v3 whole, which is shorter than its diff:
```python
import jax
import jax.numpy as jnp
from jax import lax
from jax.experimental import pallas as pl
from jax.experimental.pallas import tpu as pltpu
from jax.sharding import PartitionSpec as P

BF = jnp.bfloat16
F32 = jnp.float32
T, D, FF = 4096, 960, 2560
SH = FF // 4
HB = FF // 2
TB = 512
NT = T // TB
NB = 256
RC = 240
NK = 3 * D // RC
DH = D // 2
KY = 8
GB = 512
VM = 63 * 1024 * 1024
ANY = pl.BlockSpec(memory_space=pl.ANY)
DMA = pltpu.SemaphoreType.DMA


def rcopy(src, dst, ss, rs, dev):
    return pltpu.make_async_remote_copy(src_ref=src, dst_ref=dst, send_sem=ss, recv_sem=rs,
                                        device_id=dev, device_id_type=pl.DeviceIdType.MESH)


def main_kernel(x, dy, w1s, w3s, w2s, g,
                h, da, db, dxp, dx, rn, ra, gs, gt, ys,
                wo, wn, xb, yb, xt, yt, hb, dab, dbb, pb, ob, xs, xr, nb, ab, gb,
                wl, wcs, wcr, wxs, wxr, wys, wyr, w1fs, w1fr, w2fs, w2fr,
                gns, gnr, gas, gar, xss, xsr, yss, ysr, ldn, lda, gst, xsem, hsem, psem, osem):
    d, o, c = lax.axis_index("dp"), lax.axis_index("fo"), lax.axis_index("fi")
    cdev, xdev, ydev = (d, o, 1 - c), (d, 1 - o, c), (1 - d, o, c)
    shards = (w1s, w3s, w2s)

    def cols(cc):
        return pl.ds(pl.multiple_of(cc * SH, 128), SH)

    def gcols(oo, cc):
        return pl.ds(pl.multiple_of((oo * 2 + cc) * SH, 128), SH)

    def rows(k):
        return pl.ds(pl.multiple_of(k * RC, 16), RC)

    def half(dd):
        return pl.ds(pl.multiple_of(dd * DH, 16), DH)

    bar = pltpu.get_barrier_semaphore()
    for dev in (cdev, xdev, ydev):
        pl.semaphore_signal(bar, inc=1, device_id=dev, device_id_type=pl.DeviceIdType.MESH)
    pl.semaphore_wait(bar, 3)

    def c_own(m):
        return rcopy(shards[m], wo.at[m, :, cols(c)], wcs.at[m], wcr.at[m], cdev)

    def x_own(m):
        return rcopy(shards[m].at[half(d), :], wn.at[m, half(d), cols(c)], wxs.at[m], wxr.at[m], xdev)

    def y_fwd(m):
        v = wn.at[m, half(d), cols(c)]
        return rcopy(v, v, wys.at[m], wyr.at[m], ydev)

    def c_fwd1(m):
        v = wn.at[m, half(d), cols(c)]
        return rcopy(v, v, w1fs.at[m], w1fr.at[m], cdev)

    def c_fwd2(m):
        v = wn.at[m, half(1 - d), cols(c)]
        return rcopy(v, v, w2fs.at[m], w2fr.at[m], cdev)

    def l_own(m):
        return pltpu.make_async_copy(shards[m], wo.at[m, :, cols(c)], wl.at[m])

    def g_n(k):
        return rcopy(g.at[rows(k), gcols(1 - o, 1 - c)], rn.at[rows(k), :], gns.at[k], gnr.at[k], cdev)

    def g_a(k):
        return rcopy(g.at[rows(k), gcols(o, 1 - c)], ra.at[rows(k), :], gas.at[k], gar.at[k], cdev)

    def x_sum(k):
        return rcopy(xs.at[k], xr.at[k], xss.at[k], xsr.at[k], xdev)

    def loads(k, oo, rec, buf, sem):
        q = k % 2
        return (pltpu.make_async_copy(g.at[rows(k), gcols(oo, c)], buf.at[q, 0], sem.at[q, 0]),
                pltpu.make_async_copy(rec.at[rows(k), :], buf.at[q, 1], sem.at[q, 1]))

    def load_n(k):
        return loads(k, 1 - o, rn, nb, ldn)

    def load_a(k):
        return loads(k, o, ra, ab, lda)

    def start_n(k):
        g_n(k).wait_recv()
        for cp in load_n(k):
            cp.start()

    def start_a(k):
        g_a(k).wait_recv()
        for cp in load_a(k):
            cp.start()

    def g_out(k):
        return pltpu.make_async_copy(gb.at[k], gs.at[rows(k), :], gst.at[k])

    def t_out(k):
        return pltpu.make_async_copy(gb.at[k], gt.at[rows(k - KY), :], gst.at[k])

    def y_sum(k):
        return rcopy(gb.at[k], ys.at[rows(k), :], yss.at[k], ysr.at[k], ydev)

    def pair_sum(buf, q):
        return buf[q, 0].astype(BF).astype(F32) + buf[q, 1].astype(BF).astype(F32)

    def sum1(k, q):
        xs[k] = pair_sum(nb, q).astype(BF)

    def wait_a(k):
        for cp in load_a(k):
            cp.wait()
        x_sum(k).wait_recv()

    def sum2(k, q):
        gb[k] = (pair_sum(ab, q) + xr[k].astype(F32)).astype(BF)

    def share(k):
        g_out(k).start()
        y_sum(k).start()

    def tiles(j):
        q = j % 2
        t = pl.ds(pl.multiple_of((j % NT) * TB, 128), TB)
        return (pltpu.make_async_copy(x.at[:, t], xb.at[q], xsem.at[q, 0]),
                pltpu.make_async_copy(dy.at[:, t], yb.at[q], xsem.at[q, 1]))

    def acts(p, i):
        q = i % 2
        t = pl.ds(pl.multiple_of(i * TB, 128), TB)
        hc = pl.ds(pl.multiple_of((o if p == 0 else 1 - o) * HB, 128), HB)
        return (pltpu.make_async_copy(hb.at[q], h.at[t, hc], hsem.at[q, 0]),
                pltpu.make_async_copy(dab.at[q], da.at[t, hc], hsem.at[q, 1]),
                pltpu.make_async_copy(dbb.at[q], db.at[t, hc], hsem.at[q, 2]))

    def tok(i):
        return pl.ds(pl.multiple_of(i * TB, 128), TB)

    def p_out(i):
        return pltpu.make_async_copy(pb.at[i % 2], dxp.at[:, tok(i)], psem.at[0, i % 2])

    def p_in(i):
        return pltpu.make_async_copy(dxp.at[:, tok(i)], pb.at[i % 2], psem.at[1, i % 2])

    def d_out(i):
        return pltpu.make_async_copy(ob.at[i % 2], dx.at[:, tok(i)], osem.at[i % 2])

    def transpose(q):
        xt[...] = xb[q].T
        yt[...] = yb[q].T

    for m in range(3):
        c_own(m).start()
        l_own(m).start()
    for m in range(3):
        x_own(m).start()
    for t in (0, 1):
        for cp in tiles(t):
            cp.start()
    for cp in tiles(0):
        cp.wait()
    transpose(0)
    for m in range(3):
        l_own(m).wait()
        c_own(m).wait_recv()

    @pl.loop(0, NK)
    def _(k):
        g_n(k).start()

    @pl.loop(0, NK)
    def _(k):
        g_a(k).start()

    def step(p, i):
        j = p * NT + i
        q = i % 2
        w = (wo, wn)[p]

        def next_tile():
            for cp in tiles(j + 1):
                cp.wait()

        def start_tile():
            for cp in tiles(j + 2):
                cp.start()

        def free():
            for cp in acts(p, i):
                cp.wait()

        def wait_n():
            for cp in load_n(j - 2):
                cp.wait()

        if p == 0:
            next_tile()
            start_tile()
            for m, (s1, s2) in enumerate(((2, 5), (4, 7), (5, 8))):
                @pl.when(j == s1)
                def _():
                    x_own(m).wait_recv()
                    y_fwd(m).start()
                    c_fwd1(m).start()

                if s2 < 8:
                    @pl.when(j == s2)
                    def _():
                        y_fwd(m).wait_recv()
                        c_fwd2(m).start()

            @pl.when(i >= 2)
            def _():
                free()
                p_out(i - 2).wait()
                wait_n()

            @pl.when(i >= 1)
            def _():
                start_n(j - 1)

            @pl.when(i >= 5)
            def _():
                start_a(j - 5)

            @pl.when(i >= 6)
            def _():
                wait_a(j - 6)
                sum2(j - 6, q)
                share(j - 6)
        else:
            pl.when(i < NT - 1)(next_tile)
            pl.when(i < NT - 2)(start_tile)
            free()
            p_in(i).wait()

            @pl.when(i < NT - 1)
            def _():
                p_in(i + 1).start()

            @pl.when(i >= 2)
            def _():
                d_out(i - 2).wait()

            pl.when(i < NK + 2 - NT)(wait_n)

            @pl.when(i < NK + 1 - NT)
            def _():
                start_n(j - 1)

            start_a(j - 5)
            wait_a(j - 6)

        for n in range(HB // NB):
            cs = slice(n * NB, (n + 1) * NB)
            a = jnp.dot(xt[...], w[0, :, cs], preferred_element_type=F32)
            b = jnp.dot(xt[...], w[1, :, cs], preferred_element_type=F32)
            dh = jnp.dot(yt[...], w[2, :, cs], preferred_element_type=F32)
            s = jax.nn.sigmoid(a)
            sa = a * s
            hb[q, :, cs] = (sa * b).astype(BF)
            dab[q, :, cs] = (dh * b * (s * (1.0 + a * (1.0 - s)))).astype(BF)
            dbb[q, :, cs] = (dh * sa).astype(BF)

        def nt(m, v):
            return lax.dot_general(w[m], v[q], (((1,), (1,)), ((), ())), preferred_element_type=F32)

        transpose(1 - q)
        sum1((j + NK) % (NK + 2), q)
        if p == 0:
            pb[q] = nt(0, dab) + nt(1, dbb)
            p_out(i).start()
        else:
            sum2(j - 6, q)
            ob[q] = (pb[q] + nt(0, dab) + nt(1, dbb)).astype(BF)
            d_out(i).start()
        for cp in acts(p, i):
            cp.start()
        if p == 0:
            @pl.when(i >= 2)
            def _():
                x_sum(j - 2).start()
        else:
            @pl.when(i < NK + 2 - NT)
            def _():
                x_sum(j - 2).start()

            @pl.when(j - 6 < KY)
            def _():
                share(j - 6)

            @pl.when(j - 6 >= KY)
            def _():
                t_out(j - 6).start()

    @pl.loop(0, NT)
    def _(i):
        step(0, i)

    for i in (NT - 2, NT - 1):
        p_out(i).wait()
    p_in(0).start()
    y_fwd(2).wait_recv()
    c_fwd2(2).start()
    for m in range(3):
        c_fwd1(m).wait_recv()
        c_fwd2(m).wait_recv()

    @pl.loop(0, NT)
    def _(i):
        step(1, i)

    start_a(NK - 1)
    for k in (NK - 2, NK - 1):
        wait_a(k)
        sum2(k, k % 2)
        t_out(k).start()
    for i in (NT - 2, NT - 1):
        d_out(i).wait()
        for cp in acts(1, i):
            cp.wait()
    for m in range(3):
        for f in (c_own, x_own, y_fwd, c_fwd1, c_fwd2):
            f(m).wait_send()

    @pl.loop(0, NK)
    def _(k):
        g_n(k).wait_send()
        g_a(k).wait_send()
        x_sum(k).wait_send()

    @pl.loop(0, KY)
    def _(k):
        g_out(k).wait()
        y_sum(k).wait()

    for k in range(KY, NK):
        t_out(k).wait()


def main_call(xT, dyT, w1s, w3s, w2sT, g2):
    def out(n, m, t=BF):
        return jax.ShapeDtypeStruct((n, m), t)

    V = pltpu.VMEM
    return pl.pallas_call(
        main_kernel,
        out_shape=(out(T, FF), out(T, FF), out(T, FF), out(D, T, F32), out(D, T),
                   out(3 * D, SH, F32), out(3 * D, SH, F32),
                   out(KY * RC, SH), out((NK - KY) * RC, SH), out(KY * RC, SH)),
        in_specs=[ANY] * 6,
        out_specs=(ANY,) * 10,
        scratch_shapes=[
            V((3, D, HB), BF), V((3, D, HB), BF),
            V((2, D, TB), BF), V((2, D, TB), BF), V((TB, D), BF), V((TB, D), BF),
            V((2, TB, HB), BF), V((2, TB, HB), BF), V((2, TB, HB), BF),
            V((2, D, TB), F32), V((2, D, TB), BF),
            V((NK + 2, RC, SH), BF), V((NK, RC, SH), BF),
            V((2, 2, RC, SH), F32), V((2, 2, RC, SH), F32), V((NK, RC, SH), BF),
        ] + [DMA((3,))] * 11 + [DMA((NK,))] * 6 + [DMA((KY,))] * 2
        + [DMA((2, 2)), DMA((2, 2)), DMA((NK,)), DMA((2, 2)), DMA((2, 3)), DMA((2, 2)), DMA((2,))],
        compiler_params=pltpu.CompilerParams(vmem_limit_bytes=VM, collective_id=0, has_side_effects=True),
        cost_estimate=pl.CostEstimate(flops=10 * T * D * FF, bytes_accessed=200_000_000, transcendentals=T * FF),
    )(xT, dyT, w1s, w3s, w2sT, g2)


def gw_kernel(x_ref, dy_ref, da_ref, db_ref, h_ref, dxi_ref, g_ref, y_ref, o_ref, dxo_ref, s_ref, lhs, rb, lsem, rsem):
    nj = FF // GB
    s = pl.program_id(0)
    q = s % 2
    cx = pltpu.make_async_copy(x_ref, lhs.at[0], lsem.at[0])
    cy = pltpu.make_async_copy(dy_ref, lhs.at[1], lsem.at[1])

    def rhs(src, t):
        c = pl.ds(pl.multiple_of((t % nj) * GB, 128), GB)
        return pltpu.make_async_copy(src.at[:, c], rb.at[t % 2], rsem.at[t % 2])

    @pl.when(s == 0)
    def _():
        rhs(da_ref, s).start()
        cx.start()
        cx.wait()
        cy.start()

    for k, src in enumerate((da_ref, db_ref, h_ref)):
        @pl.when((s + 1 >= k * nj) & (s + 1 < (k + 1) * nj))
        def _():
            rhs(src, s + 1).start()

    @pl.when(s == 2 * nj)
    def _():
        cy.wait()

    rhs(da_ref, s).wait()
    o_ref[0, 0] = jnp.dot(lhs[s // (2 * nj)], rb[q], preferred_element_type=F32)
    dxo_ref[...] = dxi_ref[...]
    s_ref[...] = g_ref[...].astype(F32) + y_ref[...].astype(F32)


def gw_call(xT, dyT, da, db, h, dxi, gs, ys):
    nj = FF // GB
    dspec = pl.BlockSpec((D, TB), lambda s: (0, jnp.minimum(s, NT - 1)))
    gspec = pl.BlockSpec((RC, SH), lambda s: (jnp.minimum(s, KY - 1), 0))
    return pl.pallas_call(
        gw_kernel,
        out_shape=(jax.ShapeDtypeStruct((1, 3, D, FF), F32), jax.ShapeDtypeStruct((D, T), BF),
                   jax.ShapeDtypeStruct((3 * D, SH), F32)),
        grid=(3 * nj,),
        in_specs=[ANY] * 5 + [dspec, gspec, gspec],
        out_specs=(pl.BlockSpec((1, 1, D, GB), lambda s: (0, s // nj, 0, s % nj)), dspec, gspec),
        scratch_shapes=[pltpu.VMEM((2, D, T), BF), pltpu.VMEM((2, T, GB), BF), DMA((2,)), DMA((2,))],
        compiler_params=pltpu.CompilerParams(vmem_limit_bytes=VM),
        cost_estimate=pl.CostEstimate(flops=6 * T * D * FF, bytes_accessed=4 * T * D + 6 * T * FF + 12 * D * FF,
                                      transcendentals=0),
    )(xT, dyT, da, db, h, dxi, gs, ys)


def final_kernel(g_ref, y_ref, _, o_ref):
    o_ref[...] = g_ref[...].astype(F32) + y_ref[...].astype(F32)


def final_call(gt, yt, acc):
    rb, first = 480, KY * RC // 480
    spec = pl.BlockSpec((rb, SH), lambda i: (i, 0))
    return pl.pallas_call(
        final_kernel,
        out_shape=jax.ShapeDtypeStruct((3 * D, SH), F32),
        grid=((NK - KY) * RC // rb,), in_specs=[spec, spec, ANY],
        out_specs=pl.BlockSpec((rb, SH), lambda i: (i + first, 0)),
        input_output_aliases={2: 0},
        compiler_params=pltpu.CompilerParams(vmem_limit_bytes=16 * 1024 * 1024),
        cost_estimate=pl.CostEstimate(flops=D * SH, bytes_accessed=8 * D * SH, transcendentals=0),
    )(gt, yt, acc)


def solution(mesh):
    grp = ("fo", "fi")
    alla = ("dp", "fo", "fi")
    flip = [(0, 1), (1, 0)]

    def local(x, dy, w1s, w3s, w2s, g):
        xT, dyT = x.T, dy.T
        h, da, db, _, dxT, _, _, gs, gt, ys = main_call(xT, dyT, w1s, w3s, w2s.T, g.reshape(3 * D, FF))
        yt = lax.ppermute(gt, "dp", flip)
        dwl, dxT, dwn = gw_call(xT, dyT, da, db, h, dxT, gs, ys)
        yt, dwn = lax.optimization_barrier((yt, dwn))
        dwn = final_call(gt, yt, dwn).reshape(3, D, SH)
        return dxT.T, dwn, dwl

    return jax.shard_map(
        local, mesh=mesh,
        in_specs=(P(alla, None), P(alla, None), P(None, grp), P(None, grp), P(grp, None),
                  P(alla, None, None, None)),
        out_specs=(P(alla, None), P(None, None, grp), P(alla, None, None, None)),
        check_vma=False)
```

time: 240 us -> 217 us (0.904)
  Pallas kernels: 229 us -> 213 us
  local copies, waits for them, and re-layouts: 5.27 us -> 1.28 us
  waiting for transfers between devices: 3.04 us -> 0.01 us
    pallas_call x2, Pallas kernels: 222 us -> 211 us  [the longest x1 137 us: main_call(): pl.pallas_call(main_kernel, out_shape=(out(T, FF), out(T, FF), out(T, FF)...]
    pallas_call x1, Pallas kernels: 7.39 us -> 2.63 us  [final_call(): pl.pallas_call(final_kernel, out_shape=jax.ShapeDtypeStruct((3 * D, SH),...]
    unnamed x5 -> x2, local copies, waits for them, and re-layouts: 5.27 us -> 1.28 us
    ppermute x1, waiting for transfers between devices: 3.04 us -> 0.01 us  [local(): yt = lax.ppermute(gt, 'dp', flip)]
  transfers between devices with their start and end apart: 1 -> 1, of which waited for: 1 -> 0; matrix products, arithmetic and copies ran while one was open for 0% -> 0% of each run, Pallas kernels for 32% -> 34%
where the time goes in v3:
time: 217 us
  Pallas kernels  213 us (98%)
    pallas_call x1, Pallas kernels, main_call(): pl.pallas_call(main_kernel, out_shape=(out(T, FF), out(T, FF), out(T, FF)...  137 us
    pallas_call x1, Pallas kernels, gw_call(): pl.pallas_call(gw_kernel, out_shape=(jax.ShapeDtypeStruct((1, 3, D, FF),...  73.5 us
  transfers between devices with their start and end apart: 1, of which 0 were waited for; matrix products, arithmetic and copies ran while one was open for 0% of the time, Pallas kernels for 34%

profile of v3, /device:TPU:0, one launch (start us, length us, event | category | flops | bytes accessed | tf_op | source)
XLA Modules:
  0.0 216.7 jit_solution(15822968590792647613)
XLA Ops:
  0.6 137.1 %shard_map.85 = (bf16[4096,2560]{1,0:T(8,128)(2,1)}, bf16[4096,2560]{1,0:T(8,128)(2,1)}, bf16[4096,2560]{1,0:T(8,128)(2,1)}, f32[960,4096]{1,0:T(8,128)}, bf16[9...) custom-call(bf16[960,4096]{1,0:T(8,128)(2,1)} %bitcast.8, ...), custom_call_target="tpu_custom_call" | custom-call | flops 100663296000 | bytes 200000000 | tf_op jit(solution)/shard_map/pallas_call | solution.py:359
  137.7 1.5 collective-permute-start
  139.2 73.5 %shard_map.86 = (f32[1,3,960,2560]{3,2,1,0:T(8,128)}, bf16[960,4096]{1,0:T(8,128)(2,1)}, f32[2880,640]{1,0:T(8,128)}) custom-call(bf16[960,4096]{1,0:T(8,128)(2,1)} %bitcast.9, bf16[960,4096]{1,0:T(8,128)(2,1)} %bitcast.11, bf16[4096,2560]{1,0:T(8,128)(2,1)} %get-tuple-element.15.da_ref, bf16[4096,2560]{1,0:T(8,128)(2,1)} %get-tuple-element.16.db_ref, ...), custom_call_target="tpu_custom_call" | custom-call | flops 60397977600 | bytes 108134400 | tf_op jit(solution)/shard_map/pallas_call | solution.py:417
  212.8 0.0 collective-permute-done.y_ref
  212.8 0.0 copy-start
  212.8 1.3 copy-done
  214.1 2.6 %shard_map.87 = f32[2880,640]{1,0:T(8,128)} custom-call(bf16[960,640]{1,0:T(8,128)(2,1)S(1)} %copy-done, bf16[960,640]{1,0:T(8,128)(2,1)} %collective-permute-done.y_ref, f32[2880,640]{1,0:T(8,128)} %get-tuple-element.25._), custom_call_target="tpu_custom_call", output_to_operand_aliasing={{}: (2, {})} | custom-call | flops 614400 | bytes 4915200 | tf_op jit(solution)/shard_map/pallas_call | solution.py:438
Async XLA Ops:
  137.7 75.0 %collective-permute-start = (bf16[960,640]{1,0:T(8,128)(2,1)}, bf16[960,640]{1,0:T(8,128)(2,1)}, u32[]{:S(2)}, u32[]{:S(2)}) collective-permute-start(bf16[960,640]{1,0:T(8,128)(2,1)} %get-tuple-element.22.g_ref), channel_id=1, source_target_pairs={{0,4},{4,0},{1,5},{5,1},{2,6},{6,2},{3,7},{7,3}} | collective-permute-start | bytes 3686408 | tf_op jit(solution)/shard_map/ppermute | solution.py:457
  212.8 1.3 copy-start

commit v4 on v3

--- a/solution.py
+++ b/solution.py
@@ -29,10 +29,10 @@
 
 
 def main_kernel(x, dy, w1s, w3s, w2s, g,
-                h, da, db, dxp, dx, rn, ra, gs, gt, ys,
+                h, da, db, dxp, dx, rn, ra, gs, ys, ap, bp,
                 wo, wn, xb, yb, xt, yt, hb, dab, dbb, pb, ob, xs, xr, nb, ab, gb,
                 wl, wcs, wcr, wxs, wxr, wys, wyr, w1fs, w1fr, w2fs, w2fr,
-                gns, gnr, gas, gar, xss, xsr, yss, ysr, ldn, lda, gst, xsem, hsem, psem, osem):
+                gns, gnr, gas, gar, xss, xsr, yss, ysr, ldn, lda, gst, bst, xsem, hsem, psem, osem):
     d, o, c = lax.axis_index("dp"), lax.axis_index("fo"), lax.axis_index("fi")
     cdev, xdev, ydev = (d, o, 1 - c), (d, 1 - o, c), (1 - d, o, c)
     shards = (w1s, w3s, w2s)
@@ -108,8 +108,11 @@
     def g_out(k):
         return pltpu.make_async_copy(gb.at[k], gs.at[rows(k), :], gst.at[k])
 
-    def t_out(k):
-        return pltpu.make_async_copy(gb.at[k], gt.at[rows(k - KY), :], gst.at[k])
+    def a_out(k):
+        return pltpu.make_async_copy(gb.at[k], ap.at[rows(k - KY), :], gst.at[k])
+
+    def b_out(k):
+        return pltpu.make_async_copy(xs.at[k], bp.at[rows(k - KY), :], bst.at[k - KY])
 
     def y_sum(k):
         return rcopy(gb.at[k], ys.at[rows(k), :], yss.at[k], ysr.at[k], ydev)
@@ -123,10 +126,9 @@
     def wait_a(k):
         for cp in load_a(k):
             cp.wait()
-        x_sum(k).wait_recv()
-
-    def sum2(k, q):
-        gb[k] = (pair_sum(ab, q) + xr[k].astype(F32)).astype(BF)
+
+    def sum2(k, r, q):
+        gb[k] = (pair_sum(ab, q) + xr[r].astype(F32)).astype(BF)
 
     def share(k):
         g_out(k).start()
@@ -177,12 +179,12 @@
         l_own(m).wait()
         c_own(m).wait_recv()
 
-    @pl.loop(0, NK)
-    def _(k):
+    for k in range(NK - KY):
         g_n(k).start()
-
-    @pl.loop(0, NK)
-    def _(k):
+        g_a(KY + k).start()
+    for k in range(NK - KY, NK):
+        g_n(k).start()
+    for k in range(KY):
         g_a(k).start()
 
     def step(p, i):
@@ -232,6 +234,14 @@
             def _():
                 start_n(j - 1)
 
+            @pl.when((i >= 2) & (i < 2 + NK - KY))
+            def _():
+                wait_a(j + 6)
+
+            @pl.when((i >= 1) & (i < 1 + NK - KY))
+            def _():
+                start_a(j + 7)
+
             @pl.when(i >= 5)
             def _():
                 start_a(j - 5)
@@ -239,7 +249,8 @@
             @pl.when(i >= 6)
             def _():
                 wait_a(j - 6)
-                sum2(j - 6, q)
+                x_sum(j - 6).wait_recv()
+                sum2(j - 6, j - 6, q)
                 share(j - 6)
         else:
             pl.when(i < NT - 1)(next_tile)
@@ -261,8 +272,14 @@
             def _():
                 start_n(j - 1)
 
-            start_a(j - 5)
-            wait_a(j - 6)
+            @pl.when(j < KY + 5)
+            def _():
+                start_a(j - 5)
+
+            @pl.when(j < KY + 6)
+            def _():
+                wait_a(j - 6)
+                x_sum(j - 6).wait_recv()
 
         for n in range(HB // NB):
             cs = slice(n * NB, (n + 1) * NB)
@@ -281,10 +298,11 @@
         transpose(1 - q)
         sum1((j + NK) % (NK + 2), q)
         if p == 0:
+            gb[j + 6] = pair_sum(ab, q).astype(BF)
             pb[q] = nt(0, dab) + nt(1, dbb)
             p_out(i).start()
         else:
-            sum2(j - 6, q)
+            sum2(j - 6 + (NK - KY) * (j // (KY + 6)), (j - 6) % KY, q)
             ob[q] = (pb[q] + nt(0, dab) + nt(1, dbb)).astype(BF)
             d_out(i).start()
         for cp in acts(p, i):
@@ -293,18 +311,22 @@
             @pl.when(i >= 2)
             def _():
                 x_sum(j - 2).start()
+
+            @pl.when((i >= 2) & (i < 2 + NK - KY))
+            def _():
+                a_out(j + 6).start()
         else:
-            @pl.when(i < NK + 2 - NT)
+            @pl.when(j < KY + 2)
             def _():
                 x_sum(j - 2).start()
 
-            @pl.when(j - 6 < KY)
+            @pl.when((j >= KY + 2) & (j < NK + 2))
+            def _():
+                b_out(j - 2).start()
+
+            @pl.when(j < KY + 6)
             def _():
                 share(j - 6)
-
-            @pl.when(j - 6 >= KY)
-            def _():
-                t_out(j - 6).start()
 
     @pl.loop(0, NT)
     def _(i):
@@ -323,11 +345,6 @@
     def _(i):
         step(1, i)
 
-    start_a(NK - 1)
-    for k in (NK - 2, NK - 1):
-        wait_a(k)
-        sum2(k, k % 2)
-        t_out(k).start()
     for i in (NT - 2, NT - 1):
         d_out(i).wait()
         for cp in acts(1, i):
@@ -340,15 +357,16 @@
     def _(k):
         g_n(k).wait_send()
         g_a(k).wait_send()
-        x_sum(k).wait_send()
 
     @pl.loop(0, KY)
     def _(k):
+        x_sum(k).wait_send()
         g_out(k).wait()
         y_sum(k).wait()
 
     for k in range(KY, NK):
-        t_out(k).wait()
+        a_out(k).wait()
+        b_out(k).wait()
 
 
 def main_call(xT, dyT, w1s, w3s, w2sT, g2):
@@ -360,18 +378,18 @@
         main_kernel,
         out_shape=(out(T, FF), out(T, FF), out(T, FF), out(D, T, F32), out(D, T),
                    out(3 * D, SH, F32), out(3 * D, SH, F32),
-                   out(KY * RC, SH), out((NK - KY) * RC, SH), out(KY * RC, SH)),
+                   out(KY * RC, SH), out(KY * RC, SH), out((NK - KY) * RC, SH), out((NK - KY) * RC, SH)),
         in_specs=[ANY] * 6,
-        out_specs=(ANY,) * 10,
+        out_specs=(ANY,) * 11,
         scratch_shapes=[
             V((3, D, HB), BF), V((3, D, HB), BF),
             V((2, D, TB), BF), V((2, D, TB), BF), V((TB, D), BF), V((TB, D), BF),
             V((2, TB, HB), BF), V((2, TB, HB), BF), V((2, TB, HB), BF),
             V((2, D, TB), F32), V((2, D, TB), BF),
-            V((NK + 2, RC, SH), BF), V((NK, RC, SH), BF),
-            V((2, 2, RC, SH), F32), V((2, 2, RC, SH), F32), V((NK, RC, SH), BF),
-        ] + [DMA((3,))] * 11 + [DMA((NK,))] * 6 + [DMA((KY,))] * 2
-        + [DMA((2, 2)), DMA((2, 2)), DMA((NK,)), DMA((2, 2)), DMA((2, 3)), DMA((2, 2)), DMA((2,))],
+            V((NK + 2, RC, SH), BF), V((KY, RC, SH), BF),
+            V((2, 2, RC, SH), F32), V((2, 2, RC, SH), F32), V((NK + 2, RC, SH), BF),
+        ] + [DMA((3,))] * 11 + [DMA((NK,))] * 4 + [DMA((KY,))] * 4
+        + [DMA((2, 2)), DMA((2, 2)), DMA((NK,)), DMA((NK - KY,)), DMA((2, 2)), DMA((2, 3)), DMA((2, 2)), DMA((2,))],
         compiler_params=pltpu.CompilerParams(vmem_limit_bytes=VM, collective_id=0, has_side_effects=True),
         cost_estimate=pl.CostEstimate(flops=10 * T * D * FF, bytes_accessed=200_000_000, transcendentals=T * FF),
     )(xT, dyT, w1s, w3s, w2sT, g2)
@@ -428,22 +446,22 @@
     )(xT, dyT, da, db, h, dxi, gs, ys)
 
 
-def final_kernel(g_ref, y_ref, _, o_ref):
-    o_ref[...] = g_ref[...].astype(F32) + y_ref[...].astype(F32)
-
-
-def final_call(gt, yt, acc):
+def final_kernel(a_ref, x_ref, y_ref, z_ref, _, o_ref):
+    o_ref[...] = (a_ref[...].astype(F32) + x_ref[...].astype(F32)) + (y_ref[...].astype(F32) + z_ref[...].astype(F32))
+
+
+def final_call(terms, acc):
     rb, first = 480, KY * RC // 480
     spec = pl.BlockSpec((rb, SH), lambda i: (i, 0))
     return pl.pallas_call(
         final_kernel,
         out_shape=jax.ShapeDtypeStruct((3 * D, SH), F32),
-        grid=((NK - KY) * RC // rb,), in_specs=[spec, spec, ANY],
+        grid=((NK - KY) * RC // rb,), in_specs=[spec] * 4 + [ANY],
         out_specs=pl.BlockSpec((rb, SH), lambda i: (i + first, 0)),
-        input_output_aliases={2: 0},
-        compiler_params=pltpu.CompilerParams(vmem_limit_bytes=16 * 1024 * 1024),
+        input_output_aliases={4: 0},
+        compiler_params=pltpu.CompilerParams(vmem_limit_bytes=VM),
         cost_estimate=pl.CostEstimate(flops=D * SH, bytes_accessed=8 * D * SH, transcendentals=0),
-    )(gt, yt, acc)
+    )(*terms, acc)
 
 
 def solution(mesh):
@@ -453,11 +471,12 @@
 
     def local(x, dy, w1s, w3s, w2s, g):
         xT, dyT = x.T, dy.T
-        h, da, db, _, dxT, _, _, gs, gt, ys = main_call(xT, dyT, w1s, w3s, w2s.T, g.reshape(3 * D, FF))
-        yt = lax.ppermute(gt, "dp", flip)
+        h, da, db, _, dxT, _, _, gs, ys, ap, bp = main_call(xT, dyT, w1s, w3s, w2s.T, g.reshape(3 * D, FF))
+        far = [lax.ppermute(bp, "fo", flip), lax.ppermute(ap, "dp", flip),
+               lax.ppermute(bp, ("dp", "fo"), [(k, 3 - k) for k in range(4)])]
         dwl, dxT, dwn = gw_call(xT, dyT, da, db, h, dxT, gs, ys)
-        yt, dwn = lax.optimization_barrier((yt, dwn))
-        dwn = final_call(gt, yt, dwn).reshape(3, D, SH)
+        far, dwn = lax.optimization_barrier((far, dwn))
+        dwn = final_call([ap] + far, dwn).reshape(3, D, SH)
         return dxT.T, dwn, dwl
 
     return jax.shard_map(

time: 217 us -> 219 us (level)
  transfers between devices with their start and end apart: 1 -> 3, of which waited for: 0 -> 0; matrix products, arithmetic and copies ran while one was open for 0% -> 0% of each run, Pallas kernels for 34% -> 34%
where the time goes in v4:
time: 219 us
  Pallas kernels  215 us (98%)
  starting transfers between devices  3.51 us (2%)
    pallas_call x1, Pallas kernels, main_call(): pl.pallas_call(main_kernel, out_shape=(out(T, FF), out(T, FF), out(T, FF)...  137 us
    pallas_call x1, Pallas kernels, gw_call(): pl.pallas_call(gw_kernel, out_shape=(jax.ShapeDtypeStruct((1, 3, D, FF),...  73.5 us
  transfers between devices with their start and end apart: 3, of which 0 were waited for; matrix products, arithmetic and copies ran while one was open for 0% of the time, Pallas kernels for 34%

profile of v4, /device:TPU:0, one launch (start us, length us, event | category | flops | bytes accessed | tf_op | source)
XLA Modules:
  0.0 218.8 jit_solution(9061352824172508239)
XLA Ops:
  0.6 137.4 %shard_map.85 = (bf16[4096,2560]{1,0:T(8,128)(2,1)}, bf16[4096,2560]{1,0:T(8,128)(2,1)}, bf16[4096,2560]{1,0:T(8,128)(2,1)}, f32[960,4096]{1,0:T(8,128)}, bf16[9...) custom-call(bf16[960,4096]{1,0:T(8,128)(2,1)} %bitcast.8, ...), custom_call_target="tpu_custom_call" | custom-call | flops 100663296000 | bytes 200000000 | tf_op jit(solution)/shard_map/pallas_call | solution.py:377
  138.0 1.4 collective-permute-start.2
  139.4 1.5 collective-permute-start
  141.0 0.5 collective-permute-start.1
  141.5 73.5 %shard_map.86 = (f32[1,3,960,2560]{3,2,1,0:T(8,128)}, bf16[960,4096]{1,0:T(8,128)(2,1)}, f32[2880,640]{1,0:T(8,128)}) custom-call(bf16[960,4096]{1,0:T(8,128)(2,1)} %bitcast.9, bf16[960,4096]{1,0:T(8,128)(2,1)} %bitcast.11, bf16[4096,2560]{1,0:T(8,128)(2,1)} %get-tuple-element.18.da_ref, bf16[4096,2560]{1,0:T(8,128)(2,1)} %get-tuple-element.19.db_ref, ...), custom_call_target="tpu_custom_call" | custom-call | flops 60397977600 | bytes 108134400 | tf_op jit(solution)/shard_map/pallas_call | solution.py:435
  215.1 0.0 collective-permute-done.1.y_ref
  215.1 0.0 collective-permute-done.2.z_ref
  215.1 0.0 collective-permute-done.x_ref
  215.1 3.7 %shard_map.87 = f32[2880,640]{1,0:T(8,128)} custom-call(bf16[960,640]{1,0:T(8,128)(2,1)} %get-tuple-element.25.a_ref, bf16[960,640]{1,0:T(8,128)(2,1)} %collective-permute-done.x_ref, bf16[960,640]{1,0:T(8,128)(2,1)} %collective-permute-done.1.y_ref, bf16[960,640]{1,0:T(8,128)(2,1)} %collective-permute-done.2.z_ref, ...), custom_call_target="tpu_custom_call", output_to_operand_aliasing={{}: (4, {})} | custom-call | flops 614400 | bytes 4915200 | tf_op jit(solution)/shard_map/pallas_call | solution.py:456
Async XLA Ops:
  138.0 77.1 %collective-permute-start.2 = (bf16[960,640]{1,0:T(8,128)(2,1)}, bf16[960,640]{1,0:T(8,128)(2,1)}, u32[]{:S(2)}, u32[]{:S(2)}) collective-permute-start(bf16[960,640]{1,0:T(8,128)(2,1)} %get-tuple-element.26), channel_id=1, source_target_pairs={{0,6},{2,4},{4,2},{6,0},{1,7},{3,5},{5,3},{7,1}} | collective-permute-start | bytes 3686408 | tf_op jit(solution)/shard_map/ppermute | solution.py:476
  139.4 75.6 %collective-permute-start = (bf16[960,640]{1,0:T(8,128)(2,1)}, bf16[960,640]{1,0:T(8,128)(2,1)}, u32[]{:S(2)}, u32[]{:S(2)}) collective-permute-start(bf16[960,640]{1,0:T(8,128)(2,1)} %get-tuple-element.26), channel_id=1, source_target_pairs={{0,2},{2,0},{1,3},{3,1},{4,6},{6,4},{5,7},{7,5}} | collective-permute-start | bytes 3686408 | tf_op jit(solution)/shard_map/ppermute | solution.py:475
  141.0 74.1 %collective-permute-start.1 = (bf16[960,640]{1,0:T(8,128)(2,1)}, bf16[960,640]{1,0:T(8,128)(2,1)}, u32[]{:S(2)}, u32[]{:S(2)}) collective-permute-start(bf16[960,640]{1,0:T(8,128)(2,1)} %get-tuple-element.25.a_ref), channel_id=1, source_target_pairs={{0,4},{4,0},{1,5},{5,1},{2,6},{6,2},{3,7},{7,3}} | collective-permute-start | bytes 3686408 | tf_op jit(solution)/shard_map/ppermute | solution.py:475

commit v5 on v3

--- a/solution.py
+++ b/solution.py
@@ -29,7 +29,7 @@
 
 
 def main_kernel(x, dy, w1s, w3s, w2s, g,
-                h, da, db, dxp, dx, rn, ra, gs, gt, ys,
+                act, dxp, dx, rn, ra, gs, gt, ys,
                 wo, wn, xb, yb, xt, yt, hb, dab, dbb, pb, ob, xs, xr, nb, ab, gb,
                 wl, wcs, wcr, wxs, wxr, wys, wyr, w1fs, w1fr, w2fs, w2fr,
                 gns, gnr, gas, gar, xss, xsr, yss, ysr, ldn, lda, gst, xsem, hsem, psem, osem):
@@ -37,8 +37,7 @@
     cdev, xdev, ydev = (d, o, 1 - c), (d, 1 - o, c), (1 - d, o, c)
     shards = (w1s, w3s, w2s)
 
-    def cols(cc):
-        return pl.ds(pl.multiple_of(cc * SH, 128), SH)
+    mine, other = slice(0, SH), slice(SH, HB)
 
     def gcols(oo, cc):
         return pl.ds(pl.multiple_of((oo * 2 + cc) * SH, 128), SH)
@@ -55,25 +54,23 @@
     pl.semaphore_wait(bar, 3)
 
     def c_own(m):
-        return rcopy(shards[m], wo.at[m, :, cols(c)], wcs.at[m], wcr.at[m], cdev)
+        return rcopy(shards[m], wo.at[m, :, other], wcs.at[m], wcr.at[m], cdev)
 
     def x_own(m):
-        return rcopy(shards[m].at[half(d), :], wn.at[m, half(d), cols(c)], wxs.at[m], wxr.at[m], xdev)
+        return rcopy(shards[m].at[half(d), :], wn.at[m, half(d), mine], wxs.at[m], wxr.at[m], xdev)
 
     def y_fwd(m):
-        v = wn.at[m, half(d), cols(c)]
+        v = wn.at[m, half(d), mine]
         return rcopy(v, v, wys.at[m], wyr.at[m], ydev)
 
     def c_fwd1(m):
-        v = wn.at[m, half(d), cols(c)]
-        return rcopy(v, v, w1fs.at[m], w1fr.at[m], cdev)
+        return rcopy(wn.at[m, half(d), mine], wn.at[m, half(d), other], w1fs.at[m], w1fr.at[m], cdev)
 
     def c_fwd2(m):
-        v = wn.at[m, half(1 - d), cols(c)]
-        return rcopy(v, v, w2fs.at[m], w2fr.at[m], cdev)
+        return rcopy(wn.at[m, half(1 - d), mine], wn.at[m, half(1 - d), other], w2fs.at[m], w2fr.at[m], cdev)
 
     def l_own(m):
-        return pltpu.make_async_copy(shards[m], wo.at[m, :, cols(c)], wl.at[m])
+        return pltpu.make_async_copy(shards[m], wo.at[m, :, mine], wl.at[m])
 
     def g_n(k):
         return rcopy(g.at[rows(k), gcols(1 - o, 1 - c)], rn.at[rows(k), :], gns.at[k], gnr.at[k], cdev)
@@ -115,10 +112,10 @@
         return rcopy(gb.at[k], ys.at[rows(k), :], yss.at[k], ysr.at[k], ydev)
 
     def pair_sum(buf, q):
-        return buf[q, 0].astype(BF).astype(F32) + buf[q, 1].astype(BF).astype(F32)
+        return buf[q, 0].astype(BF) + buf[q, 1].astype(BF)
 
     def sum1(k, q):
-        xs[k] = pair_sum(nb, q).astype(BF)
+        xs[k] = pair_sum(nb, q)
 
     def wait_a(k):
         for cp in load_a(k):
@@ -126,7 +123,7 @@
         x_sum(k).wait_recv()
 
     def sum2(k, q):
-        gb[k] = (pair_sum(ab, q) + xr[k].astype(F32)).astype(BF)
+        gb[k] = pair_sum(ab, q) + xr[k]
 
     def share(k):
         g_out(k).start()
@@ -141,10 +138,9 @@
     def acts(p, i):
         q = i % 2
         t = pl.ds(pl.multiple_of(i * TB, 128), TB)
-        hc = pl.ds(pl.multiple_of((o if p == 0 else 1 - o) * HB, 128), HB)
-        return (pltpu.make_async_copy(hb.at[q], h.at[t, hc], hsem.at[q, 0]),
-                pltpu.make_async_copy(dab.at[q], da.at[t, hc], hsem.at[q, 1]),
-                pltpu.make_async_copy(dbb.at[q], db.at[t, hc], hsem.at[q, 2]))
+        oo = o if p == 0 else 1 - o
+        return [pltpu.make_async_copy(v.at[q, :, loc], act.at[m, t, gcols(oo, cc)], hsem.at[q, m, k])
+                for m, v in enumerate((dab, dbb, hb)) for k, (loc, cc) in enumerate(((mine, c), (other, 1 - c)))]
 
     def tok(i):
         return pl.ds(pl.multiple_of(i * TB, 128), TB)
@@ -175,15 +171,18 @@
     transpose(0)
     for m in range(3):
         l_own(m).wait()
-        c_own(m).wait_recv()
-
-    @pl.loop(0, NK)
-    def _(k):
-        g_n(k).start()
-
-    @pl.loop(0, NK)
-    def _(k):
-        g_a(k).start()
+
+    def shard_in():
+        for m in range(3):
+            c_own(m).wait_recv()
+
+        @pl.loop(0, NK)
+        def _(k):
+            g_n(k).start()
+
+        @pl.loop(0, NK)
+        def _(k):
+            g_a(k).start()
 
     def step(p, i):
         j = p * NT + i
@@ -265,6 +264,8 @@
             wait_a(j - 6)
 
         for n in range(HB // NB):
+            if p == 0 and n == 2:
+                pl.when(j == 0)(shard_in)
             cs = slice(n * NB, (n + 1) * NB)
             a = jnp.dot(xt[...], w[0, :, cs], preferred_element_type=F32)
             b = jnp.dot(xt[...], w[1, :, cs], preferred_element_type=F32)
@@ -358,11 +359,11 @@
     V = pltpu.VMEM
     return pl.pallas_call(
         main_kernel,
-        out_shape=(out(T, FF), out(T, FF), out(T, FF), out(D, T, F32), out(D, T),
+        out_shape=(jax.ShapeDtypeStruct((3, T, FF), BF), out(D, T, F32), out(D, T),
                    out(3 * D, SH, F32), out(3 * D, SH, F32),
                    out(KY * RC, SH), out((NK - KY) * RC, SH), out(KY * RC, SH)),
         in_specs=[ANY] * 6,
-        out_specs=(ANY,) * 10,
+        out_specs=(ANY,) * 8,
         scratch_shapes=[
             V((3, D, HB), BF), V((3, D, HB), BF),
             V((2, D, TB), BF), V((2, D, TB), BF), V((TB, D), BF), V((TB, D), BF),
@@ -371,61 +372,125 @@
             V((NK + 2, RC, SH), BF), V((NK, RC, SH), BF),
             V((2, 2, RC, SH), F32), V((2, 2, RC, SH), F32), V((NK, RC, SH), BF),
         ] + [DMA((3,))] * 11 + [DMA((NK,))] * 6 + [DMA((KY,))] * 2
-        + [DMA((2, 2)), DMA((2, 2)), DMA((NK,)), DMA((2, 2)), DMA((2, 3)), DMA((2, 2)), DMA((2,))],
+        + [DMA((2, 2)), DMA((2, 2)), DMA((NK,)), DMA((2, 2)), DMA((2, 3, 2)), DMA((2, 2)), DMA((2,))],
         compiler_params=pltpu.CompilerParams(vmem_limit_bytes=VM, collective_id=0, has_side_effects=True),
         cost_estimate=pl.CostEstimate(flops=10 * T * D * FF, bytes_accessed=200_000_000, transcendentals=T * FF),
     )(xT, dyT, w1s, w3s, w2sT, g2)
 
 
-def gw_kernel(x_ref, dy_ref, da_ref, db_ref, h_ref, dxi_ref, g_ref, y_ref, o_ref, dxo_ref, s_ref, lhs, rb, lsem, rsem):
-    nj = FF // GB
-    s = pl.program_id(0)
-    q = s % 2
-    cx = pltpu.make_async_copy(x_ref, lhs.at[0], lsem.at[0])
-    cy = pltpu.make_async_copy(dy_ref, lhs.at[1], lsem.at[1])
-
-    def rhs(src, t):
-        c = pl.ds(pl.multiple_of((t % nj) * GB, 128), GB)
-        return pltpu.make_async_copy(src.at[:, c], rb.at[t % 2], rsem.at[t % 2])
-
-    @pl.when(s == 0)
-    def _():
-        rhs(da_ref, s).start()
-        cx.start()
-        cx.wait()
-        cy.start()
-
-    for k, src in enumerate((da_ref, db_ref, h_ref)):
-        @pl.when((s + 1 >= k * nj) & (s + 1 < (k + 1) * nj))
+def gw_kernel(x, dy, act, dxi, gs, ys, dwl, dxo, dwn, lhs, rb, ob, dv, gv, sv, xsem, fsem, ysem, rsem, osem, dsem, gsem, ssem):
+    nj, nk, ni, ns = FF // GB, 4, 7, 6
+    kc = T // nk
+
+    def col(s):
+        return pl.ds(pl.multiple_of(s % nj * GB, 128), GB)
+
+    def x_in(k):
+        return pltpu.make_async_copy(x.at[:, k * kc:(k + 1) * kc], lhs.at[0, :, k * kc:(k + 1) * kc], xsem.at[k])
+
+    def first_in(k):
+        return pltpu.make_async_copy(act.at[0, k * kc:(k + 1) * kc, 0:GB], rb.at[3, k * kc:(k + 1) * kc], fsem.at[k])
+
+    def tile_in(s, q):
+        return pltpu.make_async_copy(act.at[s // nj, :, col(s)], rb.at[q], rsem.at[q])
+
+    def tile_out(s, q):
+        return pltpu.make_async_copy(ob.at[q], dwl.at[0, s // nj, :, col(s)], osem.at[q])
+
+    def side_in(u):
+        q = u % 2
+        r = pl.ds(pl.multiple_of(u * (D // ns), 16), D // ns)
+        t = pl.ds(pl.multiple_of(u * (KY * RC // ns), 16), KY * RC // ns)
+        return (pltpu.make_async_copy(dxi.at[r, :], dv.at[q], dsem.at[0, q]),
+                pltpu.make_async_copy(gs.at[t, :], gv.at[q, 0], gsem.at[q, 0]),
+                pltpu.make_async_copy(ys.at[t, :], gv.at[q, 1], gsem.at[q, 1]))
+
+    def side_out(u):
+        q = u % 2
+        r = pl.ds(pl.multiple_of(u * (D // ns), 16), D // ns)
+        t = pl.ds(pl.multiple_of(u * (KY * RC // ns), 16), KY * RC // ns)
+        return (pltpu.make_async_copy(dv.at[q], dxo.at[r, :], dsem.at[1, q]),
+                pltpu.make_async_copy(sv.at[q], dwn.at[t, :], ssem.at[q]))
+
+    dy_in = pltpu.make_async_copy(dy, lhs.at[1], ysem)
+    for k in range(nk):
+        x_in(k).start()
+        first_in(k).start()
+    for t in (0, 1):
+        tile_in(1 + t, t).start()
+    dy_in.start()
+    for k in range(nk):
+        x_in(k).wait()
+        first_in(k).wait()
+        part = jnp.dot(lhs[0, :, k * kc:(k + 1) * kc], rb[3, k * kc:(k + 1) * kc], preferred_element_type=F32)
+        ob[1] = part if k == 0 else ob[1] + part
+    tile_out(0, 1).start()
+
+    @pl.loop(0, ni)
+    def _(u):
+        s = 1 + 2 * u
+        b = u % 2 * 2
+
+        @pl.when(u < ni - 1)
         def _():
-            rhs(src, s + 1).start()
-
-    @pl.when(s == 2 * nj)
-    def _():
-        cy.wait()
-
-    rhs(da_ref, s).wait()
-    o_ref[0, 0] = jnp.dot(lhs[s // (2 * nj)], rb[q], preferred_element_type=F32)
-    dxo_ref[...] = dxi_ref[...]
-    s_ref[...] = g_ref[...].astype(F32) + y_ref[...].astype(F32)
-
-
-def gw_call(xT, dyT, da, db, h, dxi, gs, ys):
-    nj = FF // GB
-    dspec = pl.BlockSpec((D, TB), lambda s: (0, jnp.minimum(s, NT - 1)))
-    gspec = pl.BlockSpec((RC, SH), lambda s: (jnp.minimum(s, KY - 1), 0))
+            for t in (0, 1):
+                tile_in(s + 2 + t, 2 - b + t).start()
+
+        @pl.when(u >= 2)
+        def _():
+            for cp in side_out(u - 2):
+                cp.wait()
+
+        @pl.when(u < ns)
+        def _():
+            for cp in side_in(u):
+                cp.start()
+
+        @pl.when(u >= 1)
+        def _():
+            for cp in side_in(u - 1):
+                cp.wait()
+            tile_out(s, 0).wait()
+
+        @pl.when(u == 4)
+        def _():
+            dy_in.wait()
+
+        for t in (0, 1):
+            tile_in(s + t, b + t).wait()
+        tile_out(s, 1).wait()
+        for t in (0, 1):
+            ob[t] = jnp.dot(lhs[(s + t) // (2 * nj)], rb[b + t], preferred_element_type=F32)
+            if t == 0:
+                sv[1 - u % 2] = gv[1 - u % 2, 0].astype(F32) + gv[1 - u % 2, 1].astype(F32)
+            tile_out(s + t, t).start()
+
+        @pl.when(u >= 1)
+        def _():
+            for cp in side_out(u - 1):
+                cp.start()
+
+    for cp in side_out(ns - 1):
+        cp.wait()
+    for t in (0, 1):
+        tile_out(t, t).wait()
+
+
+def gw_call(xT, dyT, act, dxi, gs, ys):
+    V, kr = pltpu.VMEM, KY * RC // 6
     return pl.pallas_call(
         gw_kernel,
         out_shape=(jax.ShapeDtypeStruct((1, 3, D, FF), F32), jax.ShapeDtypeStruct((D, T), BF),
                    jax.ShapeDtypeStruct((3 * D, SH), F32)),
-        grid=(3 * nj,),
-        in_specs=[ANY] * 5 + [dspec, gspec, gspec],
-        out_specs=(pl.BlockSpec((1, 1, D, GB), lambda s: (0, s // nj, 0, s % nj)), dspec, gspec),
-        scratch_shapes=[pltpu.VMEM((2, D, T), BF), pltpu.VMEM((2, T, GB), BF), DMA((2,)), DMA((2,))],
+        in_specs=[ANY] * 6,
+        out_specs=(ANY,) * 3,
+        scratch_shapes=[V((2, D, T), BF), V((4, T, GB), BF), V((2, D, GB), F32), V((2, D // 6, T), BF),
+                        V((2, 2, kr, SH), BF), V((2, kr, SH), F32),
+                        DMA((4,)), DMA((4,)), DMA, DMA((4,)), DMA((2,)), DMA((2, 2)), DMA((2, 2)), DMA((2,))],
         compiler_params=pltpu.CompilerParams(vmem_limit_bytes=VM),
         cost_estimate=pl.CostEstimate(flops=6 * T * D * FF, bytes_accessed=4 * T * D + 6 * T * FF + 12 * D * FF,
                                       transcendentals=0),
-    )(xT, dyT, da, db, h, dxi, gs, ys)
+    )(xT, dyT, act, dxi, gs, ys)
 
 
 def final_kernel(g_ref, y_ref, _, o_ref):
@@ -441,7 +506,7 @@
         grid=((NK - KY) * RC // rb,), in_specs=[spec, spec, ANY],
         out_specs=pl.BlockSpec((rb, SH), lambda i: (i + first, 0)),
         input_output_aliases={2: 0},
-        compiler_params=pltpu.CompilerParams(vmem_limit_bytes=16 * 1024 * 1024),
+        compiler_params=pltpu.CompilerParams(vmem_limit_bytes=VM),
         cost_estimate=pl.CostEstimate(flops=D * SH, bytes_accessed=8 * D * SH, transcendentals=0),
     )(gt, yt, acc)
 
@@ -453,9 +518,9 @@
 
     def local(x, dy, w1s, w3s, w2s, g):
         xT, dyT = x.T, dy.T
-        h, da, db, _, dxT, _, _, gs, gt, ys = main_call(xT, dyT, w1s, w3s, w2s.T, g.reshape(3 * D, FF))
+        act, _, dxT, _, _, gs, gt, ys = main_call(xT, dyT, w1s, w3s, w2s.T, g.reshape(3 * D, FF))
         yt = lax.ppermute(gt, "dp", flip)
-        dwl, dxT, dwn = gw_call(xT, dyT, da, db, h, dxT, gs, ys)
+        dwl, dxT, dwn = gw_call(xT, dyT, act, dxT, gs, ys)
         yt, dwn = lax.optimization_barrier((yt, dwn))
         dwn = final_call(gt, yt, dwn).reshape(3, D, SH)
         return dxT.T, dwn, dwl

time: 217 us -> 221 us (1.018)
  Pallas kernels: 213 us -> 219 us
    pallas_call x1, Pallas kernels: 73.5 us -> 80.2 us  [gw_call(): pl.pallas_call(gw_kernel, out_shape=(jax.ShapeDtypeStruct((1, 3, D, FF),...]
  transfers between devices with their start and end apart: 1 -> 1, of which waited for: 0 -> 0; matrix products, arithmetic and copies ran while one was open for 0% -> 0% of each run, Pallas kernels for 34% -> 36%
where the time goes in v5:
time: 221 us
  Pallas kernels  219 us (99%)
    pallas_call x1, Pallas kernels, main_call(): pl.pallas_call(main_kernel, out_shape=(jax.ShapeDtypeStruct((3, T, FF), B...  136 us
    pallas_call x1, Pallas kernels, gw_call(): pl.pallas_call(gw_kernel, out_shape=(jax.ShapeDtypeStruct((1, 3, D, FF),...  80.2 us
  transfers between devices with their start and end apart: 1, of which 0 were waited for; matrix products, arithmetic and copies ran while one was open for 0% of the time, Pallas kernels for 36%

profile of v5, /device:TPU:0, one launch (start us, length us, event | category | flops | bytes accessed | tf_op | source)
XLA Modules:
  0.0 220.9 jit_solution(12254737497902743599)
XLA Ops:
  0.6 136.2 %shard_map.85 = (bf16[3,4096,2560]{2,1,0:T(8,128)(2,1)}, f32[960,4096]{1,0:T(8,128)}, bf16[960,4096]{1,0:T(8,128)(2,1)}, f32[2880,640]{1,0:T(8,128)}, f32[2880,6...) custom-call(bf16[960,4096]{1,0:T(8,128)(2,1)} %bitcast.8, ...), custom_call_target="tpu_custom_call" | custom-call | flops 100663296000 | bytes 200000000 | tf_op jit(solution)/shard_map/pallas_call | solution.py:360
  136.8 1.1 collective-permute-start
  137.9 80.2 %shard_map.86 = (f32[1,3,960,2560]{3,2,1,0:T(8,128)}, bf16[960,4096]{1,0:T(8,128)(2,1)}, f32[2880,640]{1,0:T(8,128)}) custom-call(bf16[960,4096]{1,0:T(8,128)(2,1)} %bitcast.9, bf16[960,4096]{1,0:T(8,128)(2,1)} %bitcast.11, bf16[3,4096,2560]{2,1,0:T(8,128)(2,1)} %get-tuple-element.13.act, bf16[960,4096]{1,0:T(8,128)(2,1)} %get-tuple-element.14.dxi, ...), custom_call_target="tpu_custom_call" | custom-call | flops 60397977600 | bytes 108134400 | tf_op jit(solution)/shard_map/pallas_call | solution.py:481
  218.1 0.0 collective-permute-done.y_ref
  218.1 2.8 %shard_map.87 = f32[2880,640]{1,0:T(8,128)} custom-call(bf16[960,640]{1,0:T(8,128)(2,1)} %get-tuple-element.18.g_ref, bf16[960,640]{1,0:T(8,128)(2,1)} %collective-permute-done.y_ref, f32[2880,640]{1,0:T(8,128)} %get-tuple-element.21._), custom_call_target="tpu_custom_call", output_to_operand_aliasing={{}: (2, {})} | custom-call | flops 614400 | bytes 4915200 | tf_op jit(solution)/shard_map/pallas_call | solution.py:503
Async XLA Ops:
  136.8 81.3 %collective-permute-start = (bf16[960,640]{1,0:T(8,128)(2,1)}, bf16[960,640]{1,0:T(8,128)(2,1)}, u32[]{:S(2)}, u32[]{:S(2)}) collective-permute-start(bf16[960,640]{1,0:T(8,128)(2,1)} %get-tuple-element.18.g_ref), channel_id=1, source_target_pairs={{0,4},{4,0},{1,5},{5,1},{2,6},{6,2},{3,7},{7,3}} | collective-permute-start | bytes 3686408 | tf_op jit(solution)/shard_map/ppermute | solution.py:522

commit v6 on v5

--- a/solution.py
+++ b/solution.py
@@ -405,12 +405,13 @@
                 pltpu.make_async_copy(gs.at[t, :], gv.at[q, 0], gsem.at[q, 0]),
                 pltpu.make_async_copy(ys.at[t, :], gv.at[q, 1], gsem.at[q, 1]))
 
-    def side_out(u):
-        q = u % 2
+    def dx_out(u):
         r = pl.ds(pl.multiple_of(u * (D // ns), 16), D // ns)
+        return pltpu.make_async_copy(dv.at[u % 2], dxo.at[r, :], dsem.at[1, u % 2])
+
+    def n_out(u):
         t = pl.ds(pl.multiple_of(u * (KY * RC // ns), 16), KY * RC // ns)
-        return (pltpu.make_async_copy(dv.at[q], dxo.at[r, :], dsem.at[1, q]),
-                pltpu.make_async_copy(sv.at[q], dwn.at[t, :], ssem.at[q]))
+        return pltpu.make_async_copy(sv.at[u % 2], dwn.at[t, :], ssem.at[u % 2])
 
     dy_in = pltpu.make_async_copy(dy, lhs.at[1], ysem)
     for k in range(nk):
@@ -423,8 +424,8 @@
         x_in(k).wait()
         first_in(k).wait()
         part = jnp.dot(lhs[0, :, k * kc:(k + 1) * kc], rb[3, k * kc:(k + 1) * kc], preferred_element_type=F32)
-        ob[1] = part if k == 0 else ob[1] + part
-    tile_out(0, 1).start()
+        ob[3] = part if k == 0 else ob[3] + part
+    tile_out(0, 3).start()
 
     @pl.loop(0, ni)
     def _(u):
@@ -438,8 +439,16 @@
 
         @pl.when(u >= 2)
         def _():
-            for cp in side_out(u - 2):
-                cp.wait()
+            dx_out(u - 2).wait()
+            tile_out(s, b).wait()
+
+        @pl.when(u >= 3)
+        def _():
+            n_out(u - 3).wait()
+
+        @pl.when(u >= 1)
+        def _():
+            tile_out(s, b + 1).wait()
 
         @pl.when(u < ns)
         def _():
@@ -450,7 +459,7 @@
         def _():
             for cp in side_in(u - 1):
                 cp.wait()
-            tile_out(s, 0).wait()
+            dx_out(u - 1).start()
 
         @pl.when(u == 4)
         def _():
@@ -458,21 +467,20 @@
 
         for t in (0, 1):
             tile_in(s + t, b + t).wait()
-        tile_out(s, 1).wait()
         for t in (0, 1):
-            ob[t] = jnp.dot(lhs[(s + t) // (2 * nj)], rb[b + t], preferred_element_type=F32)
+            ob[b + t] = jnp.dot(lhs[(s + t) // (2 * nj)], rb[b + t], preferred_element_type=F32)
             if t == 0:
                 sv[1 - u % 2] = gv[1 - u % 2, 0].astype(F32) + gv[1 - u % 2, 1].astype(F32)
-            tile_out(s + t, t).start()
+            tile_out(s + t, b + t).start()
 
         @pl.when(u >= 1)
         def _():
-            for cp in side_out(u - 1):
-                cp.start()
-
-    for cp in side_out(ns - 1):
-        cp.wait()
-    for t in (0, 1):
+            n_out(u - 1).start()
+
+    dx_out(ns - 1).wait()
+    for k in (ns - 2, ns - 1):
+        n_out(k).wait()
+    for t in range(4):
         tile_out(t, t).wait()
 
 
@@ -484,9 +492,9 @@
                    jax.ShapeDtypeStruct((3 * D, SH), F32)),
         in_specs=[ANY] * 6,
         out_specs=(ANY,) * 3,
-        scratch_shapes=[V((2, D, T), BF), V((4, T, GB), BF), V((2, D, GB), F32), V((2, D // 6, T), BF),
+        scratch_shapes=[V((2, D, T), BF), V((4, T, GB), BF), V((4, D, GB), F32), V((2, D // 6, T), BF),
                         V((2, 2, kr, SH), BF), V((2, kr, SH), F32),
-                        DMA((4,)), DMA((4,)), DMA, DMA((4,)), DMA((2,)), DMA((2, 2)), DMA((2, 2)), DMA((2,))],
+                        DMA((4,)), DMA((4,)), DMA, DMA((4,)), DMA((4,)), DMA((2, 2)), DMA((2, 2)), DMA((2,))],
         compiler_params=pltpu.CompilerParams(vmem_limit_bytes=VM),
         cost_estimate=pl.CostEstimate(flops=6 * T * D * FF, bytes_accessed=4 * T * D + 6 * T * FF + 12 * D * FF,
                                       transcendentals=0),

time: 221 us -> 209 us (0.946)
  Pallas kernels: 219 us -> 207 us
    pallas_call x1, Pallas kernels: 80.2 us -> 67.9 us  [gw_call(): pl.pallas_call(gw_kernel, out_shape=(jax.ShapeDtypeStruct((1, 3, D, FF),...]
  transfers between devices with their start and end apart: 1 -> 1, of which waited for: 0 -> 0; matrix products, arithmetic and copies ran while one was open for 0% -> 0% of each run, Pallas kernels for 36% -> 33%
where the time goes in v6:
time: 209 us
  Pallas kernels  207 us (99%)
    pallas_call x1, Pallas kernels, main_call(): pl.pallas_call(main_kernel, out_shape=(jax.ShapeDtypeStruct((3, T, FF), B...  136 us
    pallas_call x1, Pallas kernels, gw_call(): pl.pallas_call(gw_kernel, out_shape=(jax.ShapeDtypeStruct((1, 3, D, FF),...  67.9 us
  transfers between devices with their start and end apart: 1, of which 0 were waited for; matrix products, arithmetic and copies ran while one was open for 0% of the time, Pallas kernels for 33%

profile of v6, /device:TPU:0, one launch (start us, length us, event | category | flops | bytes accessed | tf_op | source)
XLA Modules:
  0.0 208.7 jit_solution(12748420506632695223)
XLA Ops:
  0.6 136.2 %shard_map.85 = (bf16[3,4096,2560]{2,1,0:T(8,128)(2,1)}, f32[960,4096]{1,0:T(8,128)}, bf16[960,4096]{1,0:T(8,128)(2,1)}, f32[2880,640]{1,0:T(8,128)}, f32[2880,6...) custom-call(bf16[960,4096]{1,0:T(8,128)(2,1)} %bitcast.8, ...), custom_call_target="tpu_custom_call" | custom-call | flops 100663296000 | bytes 200000000 | tf_op jit(solution)/shard_map/pallas_call | solution.py:360
  136.8 1.1 collective-permute-start
  137.9 67.9 %shard_map.86 = (f32[1,3,960,2560]{3,2,1,0:T(8,128)}, bf16[960,4096]{1,0:T(8,128)(2,1)}, f32[2880,640]{1,0:T(8,128)}) custom-call(bf16[960,4096]{1,0:T(8,128)(2,1)} %bitcast.9, bf16[960,4096]{1,0:T(8,128)(2,1)} %bitcast.11, bf16[3,4096,2560]{2,1,0:T(8,128)(2,1)} %get-tuple-element.13.act, bf16[960,4096]{1,0:T(8,128)(2,1)} %get-tuple-element.14.dxi, ...), custom_call_target="tpu_custom_call" | custom-call | flops 60397977600 | bytes 108134400 | tf_op jit(solution)/shard_map/pallas_call | solution.py:489
  205.8 0.0 collective-permute-done.y_ref
  205.8 2.8 %shard_map.87 = f32[2880,640]{1,0:T(8,128)} custom-call(bf16[960,640]{1,0:T(8,128)(2,1)} %get-tuple-element.18.g_ref, bf16[960,640]{1,0:T(8,128)(2,1)} %collective-permute-done.y_ref, f32[2880,640]{1,0:T(8,128)} %get-tuple-element.21._), custom_call_target="tpu_custom_call", output_to_operand_aliasing={{}: (2, {})} | custom-call | flops 614400 | bytes 4915200 | tf_op jit(solution)/shard_map/pallas_call | solution.py:511
Async XLA Ops:
  136.8 69.0 %collective-permute-start = (bf16[960,640]{1,0:T(8,128)(2,1)}, bf16[960,640]{1,0:T(8,128)(2,1)}, u32[]{:S(2)}, u32[]{:S(2)}) collective-permute-start(bf16[960,640]{1,0:T(8,128)(2,1)} %get-tuple-element.18.g_ref), channel_id=1, source_target_pairs={{0,4},{4,0},{1,5},{5,1},{2,6},{6,2},{3,7},{7,3}} | collective-permute-start | bytes 3686408 | tf_op jit(solution)/shard_map/ppermute | solution.py:530

commit v7 on v6

--- a/solution.py
+++ b/solution.py
@@ -81,16 +81,15 @@
     def x_sum(k):
         return rcopy(xs.at[k], xr.at[k], xss.at[k], xsr.at[k], xdev)
 
-    def loads(k, oo, rec, buf, sem):
-        q = k % 2
+    def loads(k, q, oo, rec, buf, sem):
         return (pltpu.make_async_copy(g.at[rows(k), gcols(oo, c)], buf.at[q, 0], sem.at[q, 0]),
                 pltpu.make_async_copy(rec.at[rows(k), :], buf.at[q, 1], sem.at[q, 1]))
 
     def load_n(k):
-        return loads(k, 1 - o, rn, nb, ldn)
+        return loads(k, k % 2, 1 - o, rn, nb, ldn)
 
     def load_a(k):
-        return loads(k, o, ra, ab, lda)
+        return loads(k, k % 4, o, ra, ab, lda)
 
     def start_n(k):
         g_n(k).wait_recv()
@@ -122,8 +121,8 @@
             cp.wait()
         x_sum(k).wait_recv()
 
-    def sum2(k, q):
-        gb[k] = pair_sum(ab, q) + xr[k]
+    def sum2(k):
+        gb[k] = pair_sum(ab, k % 4) + xr[k]
 
     def share(k):
         g_out(k).start()
@@ -208,7 +207,7 @@
         if p == 0:
             next_tile()
             start_tile()
-            for m, (s1, s2) in enumerate(((2, 5), (4, 7), (5, 8))):
+            for m, (s1, s2) in enumerate(((2, 5), (4, 7), (6, 8))):
                 @pl.when(j == s1)
                 def _():
                     x_own(m).wait_recv()
@@ -238,7 +237,7 @@
             @pl.when(i >= 6)
             def _():
                 wait_a(j - 6)
-                sum2(j - 6, q)
+                sum2(j - 6)
                 share(j - 6)
         else:
             pl.when(i < NT - 1)(next_tile)
@@ -261,6 +260,7 @@
                 start_n(j - 1)
 
             start_a(j - 5)
+            pl.when(i == NT - 1)(lambda: start_a(NK - 1))
             wait_a(j - 6)
 
         for n in range(HB // NB):
@@ -285,7 +285,7 @@
             pb[q] = nt(0, dab) + nt(1, dbb)
             p_out(i).start()
         else:
-            sum2(j - 6, q)
+            sum2(j - 6)
             ob[q] = (pb[q] + nt(0, dab) + nt(1, dbb)).astype(BF)
             d_out(i).start()
         for cp in acts(p, i):
@@ -294,6 +294,11 @@
             @pl.when(i >= 2)
             def _():
                 x_sum(j - 2).start()
+
+            @pl.when(i == NT - 1)
+            def _():
+                p_out(NT - 2).wait()
+                p_in(0).start()
         else:
             @pl.when(i < NK + 2 - NT)
             def _():
@@ -311,11 +316,9 @@
     def _(i):
         step(0, i)
 
-    for i in (NT - 2, NT - 1):
-        p_out(i).wait()
-    p_in(0).start()
     y_fwd(2).wait_recv()
     c_fwd2(2).start()
+    p_out(NT - 1).wait()
     for m in range(3):
         c_fwd1(m).wait_recv()
         c_fwd2(m).wait_recv()
@@ -324,10 +327,9 @@
     def _(i):
         step(1, i)
 
-    start_a(NK - 1)
     for k in (NK - 2, NK - 1):
         wait_a(k)
-        sum2(k, k % 2)
+        sum2(k)
         t_out(k).start()
     for i in (NT - 2, NT - 1):
         d_out(i).wait()
@@ -370,9 +372,9 @@
             V((2, TB, HB), BF), V((2, TB, HB), BF), V((2, TB, HB), BF),
             V((2, D, TB), F32), V((2, D, TB), BF),
             V((NK + 2, RC, SH), BF), V((NK, RC, SH), BF),
-            V((2, 2, RC, SH), F32), V((2, 2, RC, SH), F32), V((NK, RC, SH), BF),
+            V((2, 2, RC, SH), F32), V((4, 2, RC, SH), F32), V((NK, RC, SH), BF),
         ] + [DMA((3,))] * 11 + [DMA((NK,))] * 6 + [DMA((KY,))] * 2
-        + [DMA((2, 2)), DMA((2, 2)), DMA((NK,)), DMA((2, 2)), DMA((2, 3, 2)), DMA((2, 2)), DMA((2,))],
+        + [DMA((2, 2)), DMA((4, 2)), DMA((NK,)), DMA((2, 2)), DMA((2, 3, 2)), DMA((2, 2)), DMA((2,))],
         compiler_params=pltpu.CompilerParams(vmem_limit_bytes=VM, collective_id=0, has_side_effects=True),
         cost_estimate=pl.CostEstimate(flops=10 * T * D * FF, bytes_accessed=200_000_000, transcendentals=T * FF),
     )(xT, dyT, w1s, w3s, w2sT, g2)
@@ -506,7 +508,7 @@
 
 
 def final_call(gt, yt, acc):
-    rb, first = 480, KY * RC // 480
+    rb, first = RC, KY
     spec = pl.BlockSpec((rb, SH), lambda i: (i, 0))
     return pl.pallas_call(
         final_kernel,

time: 209 us -> 207 us (level)
    pallas_call x1, Pallas kernels: 136 us -> 133 us  [main_call(): pl.pallas_call(main_kernel, out_shape=(jax.ShapeDtypeStruct((3, T, FF), B...]
where the time goes in v7:
time: 207 us
  Pallas kernels  205 us (99%)
    pallas_call x1, Pallas kernels, main_call(): pl.pallas_call(main_kernel, out_shape=(jax.ShapeDtypeStruct((3, T, FF), B...  133 us
    pallas_call x1, Pallas kernels, gw_call(): pl.pallas_call(gw_kernel, out_shape=(jax.ShapeDtypeStruct((1, 3, D, FF),...  67.9 us
  transfers between devices with their start and end apart: 1, of which 0 were waited for; matrix products, arithmetic and copies ran while one was open for 0% of the time, Pallas kernels for 33%

profile of v7, /device:TPU:0, one launch (start us, length us, event | category | flops | bytes accessed | tf_op | source)
XLA Modules:
  0.0 206.9 jit_solution(4062783416757635371)
XLA Ops:
  0.6 133.3 %shard_map.85 = (bf16[3,4096,2560]{2,1,0:T(8,128)(2,1)}, f32[960,4096]{1,0:T(8,128)}, bf16[960,4096]{1,0:T(8,128)(2,1)}, f32[2880,640]{1,0:T(8,128)}, f32[2880,6...) custom-call(bf16[960,4096]{1,0:T(8,128)(2,1)} %bitcast.8, ...), custom_call_target="tpu_custom_call" | custom-call | flops 100663296000 | bytes 200000000 | tf_op jit(solution)/shard_map/pallas_call | solution.py:362
  133.9 1.1 collective-permute-start
  135.0 67.9 %shard_map.86 = (f32[1,3,960,2560]{3,2,1,0:T(8,128)}, bf16[960,4096]{1,0:T(8,128)(2,1)}, f32[2880,640]{1,0:T(8,128)}) custom-call(bf16[960,4096]{1,0:T(8,128)(2,1)} %bitcast.9, bf16[960,4096]{1,0:T(8,128)(2,1)} %bitcast.11, bf16[3,4096,2560]{2,1,0:T(8,128)(2,1)} %get-tuple-element.13.act, bf16[960,4096]{1,0:T(8,128)(2,1)} %get-tuple-element.14.dxi, ...), custom_call_target="tpu_custom_call" | custom-call | flops 60397977600 | bytes 108134400 | tf_op jit(solution)/shard_map/pallas_call | solution.py:491
  202.9 0.0 collective-permute-done.y_ref
  202.9 3.9 %shard_map.87 = f32[2880,640]{1,0:T(8,128)} custom-call(bf16[960,640]{1,0:T(8,128)(2,1)} %get-tuple-element.18.g_ref, bf16[960,640]{1,0:T(8,128)(2,1)} %collective-permute-done.y_ref, f32[2880,640]{1,0:T(8,128)} %get-tuple-element.21._), custom_call_target="tpu_custom_call", output_to_operand_aliasing={{}: (2, {})} | custom-call | flops 614400 | bytes 4915200 | tf_op jit(solution)/shard_map/pallas_call | solution.py:513
Async XLA Ops:
  133.9 69.0 %collective-permute-start = (bf16[960,640]{1,0:T(8,128)(2,1)}, bf16[960,640]{1,0:T(8,128)(2,1)}, u32[]{:S(2)}, u32[]{:S(2)}) collective-permute-start(bf16[960,640]{1,0:T(8,128)(2,1)} %get-tuple-element.18.g_ref), channel_id=1, source_target_pairs={{0,4},{4,0},{1,5},{5,1},{2,6},{6,2},{3,7},{7,3}} | collective-permute-start | bytes 3686408 | tf_op jit(solution)/shard_map/ppermute | solution.py:532

commit v8 on v7

--- a/solution.py
+++ b/solution.py
@@ -183,6 +183,8 @@
         def _(k):
             g_a(k).start()
 
+    shard_in()
+
     def step(p, i):
         j = p * NT + i
         q = i % 2
@@ -264,8 +266,6 @@
             wait_a(j - 6)
 
         for n in range(HB // NB):
-            if p == 0 and n == 2:
-                pl.when(j == 0)(shard_in)
             cs = slice(n * NB, (n + 1) * NB)
             a = jnp.dot(xt[...], w[0, :, cs], preferred_element_type=F32)
             b = jnp.dot(xt[...], w[1, :, cs], preferred_element_type=F32)
@@ -273,7 +273,7 @@
             s = jax.nn.sigmoid(a)
             sa = a * s
             hb[q, :, cs] = (sa * b).astype(BF)
-            dab[q, :, cs] = (dh * b * (s * (1.0 + a * (1.0 - s)))).astype(BF)
+            dab[q, :, cs] = (dh * b * (s + sa * (1.0 - s))).astype(BF)
             dbb[q, :, cs] = (dh * sa).astype(BF)
 
         def nt(m, v):
@@ -508,7 +508,7 @@
 
 
 def final_call(gt, yt, acc):
-    rb, first = RC, KY
+    rb, first = 2 * RC, KY // 2
     spec = pl.BlockSpec((rb, SH), lambda i: (i, 0))
     return pl.pallas_call(
         final_kernel,

time: 207 us -> 205 us (level)
  no operation moved by 1% of the time
where the time goes in v8:
time: 205 us
  Pallas kernels  204 us (100%)
    pallas_call x1, Pallas kernels, main_call(): pl.pallas_call(main_kernel, out_shape=(jax.ShapeDtypeStruct((3, T, FF), B...  133 us
    pallas_call x1, Pallas kernels, gw_call(): pl.pallas_call(gw_kernel, out_shape=(jax.ShapeDtypeStruct((1, 3, D, FF),...  67.9 us
  transfers between devices with their start and end apart: 1, of which 0 were waited for; matrix products, arithmetic and copies ran while one was open for 0% of the time, Pallas kernels for 33%

profile of v8, /device:TPU:0, one launch (start us, length us, event | category | flops | bytes accessed | tf_op | source)
XLA Modules:
  0.0 205.3 jit_solution(17787827870039577436)
XLA Ops:
  0.6 132.9 %shard_map.85 = (bf16[3,4096,2560]{2,1,0:T(8,128)(2,1)}, f32[960,4096]{1,0:T(8,128)}, bf16[960,4096]{1,0:T(8,128)(2,1)}, f32[2880,640]{1,0:T(8,128)}, f32[2880,6...) custom-call(bf16[960,4096]{1,0:T(8,128)(2,1)} %bitcast.8, ...), custom_call_target="tpu_custom_call" | custom-call | flops 100663296000 | bytes 200000000 | tf_op jit(solution)/shard_map/pallas_call | solution.py:362
  133.5 1.0 collective-permute-start
  134.5 67.9 %shard_map.86 = (f32[1,3,960,2560]{3,2,1,0:T(8,128)}, bf16[960,4096]{1,0:T(8,128)(2,1)}, f32[2880,640]{1,0:T(8,128)}) custom-call(bf16[960,4096]{1,0:T(8,128)(2,1)} %bitcast.9, bf16[960,4096]{1,0:T(8,128)(2,1)} %bitcast.11, bf16[3,4096,2560]{2,1,0:T(8,128)(2,1)} %get-tuple-element.13.act, bf16[960,4096]{1,0:T(8,128)(2,1)} %get-tuple-element.14.dxi, ...), custom_call_target="tpu_custom_call" | custom-call | flops 60397977600 | bytes 108134400 | tf_op jit(solution)/shard_map/pallas_call | solution.py:491
  202.4 0.0 collective-permute-done.y_ref
  202.4 2.8 %shard_map.87 = f32[2880,640]{1,0:T(8,128)} custom-call(bf16[960,640]{1,0:T(8,128)(2,1)} %get-tuple-element.18.g_ref, bf16[960,640]{1,0:T(8,128)(2,1)} %collective-permute-done.y_ref, f32[2880,640]{1,0:T(8,128)} %get-tuple-element.21._), custom_call_target="tpu_custom_call", output_to_operand_aliasing={{}: (2, {})} | custom-call | flops 614400 | bytes 4915200 | tf_op jit(solution)/shard_map/pallas_call | solution.py:513
Async XLA Ops:
  133.5 68.9 %collective-permute-start = (bf16[960,640]{1,0:T(8,128)(2,1)}, bf16[960,640]{1,0:T(8,128)(2,1)}, u32[]{:S(2)}, u32[]{:S(2)}) collective-permute-start(bf16[960,640]{1,0:T(8,128)(2,1)} %get-tuple-element.18.g_ref), channel_id=1, source_target_pairs={{0,4},{4,0},{1,5},{5,1},{2,6},{6,2},{3,7},{7,3}} | collective-permute-start | bytes 3686408 | tf_op jit(solution)/shard_map/ppermute | solution.py:532
